TPU v7x, 32 devices: a whole 2x2x4 slice. The times are simulated.
32 devices in a mesh: dp: 8 (over y, x, core), mp: 4 (over z).
Axes of the slice: x: 2, y: 2, z: 4, core: 2. Of those that a mesh axis runs over, the one named last changes fastest.
Arguments:
- layer_input: bfloat16 [16384, 1024], P(('dp', 'mp')), may hold values from -9 to 9
- segment_ids: int32 [8, 2048], P('dp'), may hold values from 0 to 10, as said below
- grad_out: bfloat16 [16384, 1024], P(('dp', 'mp')), may hold values from -6 to 6
- qkv_weight: bfloat16 [1024, 3, 1024], P('dp', None, 'mp'), may hold values from -0.1875 to 0.1875
- attn_weight: bfloat16 [1024, 1024], P('dp', 'mp'), may hold values from -3 to 3
- inner_weight: bfloat16 [1024, 2, 2624], P('dp', None, 'mp'), may hold values from -0.1875 to 0.1875
- outer_weight: bfloat16 [1024, 2624], P('dp', 'mp'), may hold values from -0.25 to 0.25
- attn_gain: float32 [1024], replicated, may hold values from 0.1 to 1.9
- mlp_gain: float32 [1024], replicated, may hold values from 0.1 to 1.9
Outputs:
- layer_output: bfloat16 [16384, 1024], P(('dp', 'mp'))
- input_grad: float32 [16384, 1024], P(('dp', 'mp'))
- qkv_grad: float32 [1024, 3, 1024], P('dp', None, 'mp')
- attn_grad: float32 [1024, 1024], P('dp', 'mp')
- inner_grad: float32 [1024, 2, 2624], P('dp', None, 'mp')
- outer_grad: float32 [1024, 2624], P('dp', 'mp')
- attn_gain_grad: float32 [1024], replicated
- mlp_gain_grad: float32 [1024], replicated
- rms_values: float32 [4], replicated
Inputs may be any that keep to these rules, and one draw needn't show every extreme that they name: `segment_ids`: along each sequence the numbers never fall; the nonzero ones count the documents from 1 at the sequence's start, each document of 200 to 2000 tokens; zeros fill the tail after the last document, if any. Some sequence holds 2048 // 200 documents.
All inputs are finite; a program needn't handle non-finite values.
Results may differ from a plain program's by a relative error of at most 0.018.
Values may be sent and summed in bfloat16 or wider, within the bound.
A program may use at most 192 MiB of HBM per device.

v0:
```python
import math

import jax
import jax.numpy as jnp
from jax import lax
from jax.sharding import PartitionSpec as P

HEAD_DIM = 64


NORM_EPS = 1e-05
ROPE_BASE = 160000.0
MASKED_SCORE = -1e30


def layer_norm(values, gain):
    centre = jnp.mean(values, axis=-1, keepdims=True)
    shifted = values - centre
    spread = jnp.mean(shifted * shifted, axis=-1, keepdims=True)
    return shifted * lax.rsqrt(spread + NORM_EPS) * gain


def doc_positions(segment):
    length = segment.shape[0]
    places = jnp.arange(length, dtype=jnp.int32)
    before = jnp.concatenate([jnp.full((1,), -1, jnp.int32), segment[:-1]])
    starts = jnp.where(segment != before, places, jnp.zeros_like(places))
    return places - lax.cummax(starts, axis=0)


def rope_angles(segment):
    half_dim = HEAD_DIM // 2
    frequency = jnp.exp(
        jnp.arange(half_dim, dtype=jnp.float32) * (-2.0 * math.log(ROPE_BASE) / HEAD_DIM)
    )
    return doc_positions(segment).astype(jnp.float32)[:, None] * frequency[None, :]


def rotary(values, angle):
    half_dim = values.shape[-1] // 2
    cosine = jnp.cos(angle)[:, None, :]
    sine_part = jnp.sin(angle)[:, None, :]
    first_half = values[..., :half_dim]
    second_half = values[..., half_dim:]
    return jnp.concatenate(
        [
            first_half * cosine - second_half * sine_part,
            second_half * cosine + first_half * sine_part,
        ],
        axis=-1,
    )


def gated_act(gates):
    return jax.nn.gelu(gates[:, 0], approximate=False) * gates[:, 1]


def block_masks(segment, row_start, block_rows):
    seg_rows = lax.dynamic_slice_in_dim(segment, row_start, block_rows)
    live_rows = seg_rows != 0
    allowed = (seg_rows[:, None] == segment[None, :]) & live_rows[:, None]
    return (allowed, live_rows)


def masked_scores(q_rows, key_rot, allowed, score_scale):
    scores = (
        jnp.einsum("qhe,khe->hqk", q_rows, key_rot, preferred_element_type=jnp.float32)
        * score_scale
    )
    return jnp.where(allowed[None], scores, MASKED_SCORE)


def local(
    layer_input,
    segment_ids,
    grad_out,
    qkv_weight,
    attn_weight,
    inner_weight,
    outer_weight,
    attn_gain,
    mlp_gain,
):
    row_count, feature_count = layer_input.shape
    segment = segment_ids[0]
    seq_length = segment.shape[0]
    head_cols = qkv_weight.shape[2]
    heads_here = head_cols // HEAD_DIM
    head_shape = (seq_length, heads_here, HEAD_DIM)
    score_scale = HEAD_DIM ** (-0.5)
    block_rows = min(512, seq_length)
    block_count = seq_length // block_rows
    angle = rope_angles(segment)
    my_start = lax.axis_index("mp") * row_count
    seg_mine = lax.dynamic_slice_in_dim(segment, my_start, row_count)
    live_mine = (seg_mine != 0).astype(jnp.float32)[:, None]
    tokens = layer_input.astype(jnp.float32)
    qkv_full, attn_full = (
        lax.all_gather(qkv_weight, "dp", axis=0, tiled=True),
        lax.all_gather(attn_weight, "dp", axis=0, tiled=True),
    )
    normed = layer_norm(tokens, attn_gain).astype(jnp.bfloat16)
    normed_all = lax.all_gather(normed, "mp", axis=0, tiled=True)
    qkv_all = jnp.einsum("ld,dcf->lcf", normed_all, qkv_full, preferred_element_type=jnp.float32)
    query_rot = rotary(qkv_all[:, 0].reshape(head_shape), angle).astype(jnp.bfloat16)
    key_rot = rotary(qkv_all[:, 1].reshape(head_shape), angle).astype(jnp.bfloat16)
    value_rows = qkv_all[:, 2].reshape(head_shape).astype(jnp.bfloat16)

    def forward_block(block_index):
        row_start = block_index * block_rows
        allowed, live_rows = block_masks(segment, row_start, block_rows)
        q_rows = lax.dynamic_slice_in_dim(query_rot, row_start, block_rows)
        masked = masked_scores(q_rows, key_rot, allowed, score_scale)
        row_top = jnp.where(live_rows[None, :], jnp.max(masked, axis=-1), 0.0)
        weights = jnp.exp(masked - row_top[..., None])
        row_total = jnp.where(live_rows[None, :], jnp.sum(weights, axis=-1), 1.0)
        attn_prob = (weights / row_total[..., None]).astype(jnp.bfloat16)
        mixed_heads = jnp.einsum(
            "hqk,khe->qhe", attn_prob, value_rows, preferred_element_type=jnp.float32
        )
        return (mixed_heads.astype(jnp.bfloat16), row_top, row_total)

    block_ids = jnp.arange(block_count, dtype=jnp.int32)
    mixed_heads, row_tops, row_totals = lax.map(forward_block, block_ids)
    heads_out = mixed_heads.reshape(seq_length, head_cols)
    piece_rows = heads_out
    attn_out = lax.psum_scatter(
        lax.dot_general(
            piece_rows, attn_full, (((1,), (1,)), ((), ())), preferred_element_type=jnp.float32
        ),
        "mp",
        scatter_dimension=0,
        tiled=True,
    )
    middle = tokens + attn_out
    inner_full, outer_full = (
        lax.all_gather(inner_weight, "dp", axis=0, tiled=True),
        lax.all_gather(outer_weight, "dp", axis=0, tiled=True),
    )
    inner_in = layer_norm(middle, mlp_gain).astype(jnp.bfloat16)
    inner_all = lax.all_gather(inner_in, "mp", axis=0, tiled=True)
    gates = jnp.einsum("ld,dcf->lcf", inner_all, inner_full, preferred_element_type=jnp.float32)
    hidden = gated_act(gates).astype(jnp.bfloat16)
    piece_rows = hidden
    mlp_out = lax.psum_scatter(
        lax.dot_general(
            piece_rows, outer_full, (((1,), (1,)), ((), ())), preferred_element_type=jnp.float32
        ).astype(jnp.bfloat16),
        "mp",
        scatter_dimension=0,
        tiled=True,
    ).astype(jnp.float32)
    layer_output = (middle + mlp_out).astype(jnp.bfloat16)
    squares = jnp.stack(
        [
            jnp.sum(live_mine * tokens * tokens),
            jnp.sum(live_mine * attn_out * attn_out),
            jnp.sum(live_mine * middle * middle),
            jnp.sum(live_mine * mlp_out * mlp_out),
        ]
    )
    live_count = jnp.sum(live_mine)
    grad_all = lax.all_gather(grad_out, "mp", axis=0, tiled=True)
    outer_grad = lax.dot_general(
        grad_all, hidden, (((0,), (0,)), ((), ())), preferred_element_type=jnp.float32
    )
    hidden_grad = jnp.dot(grad_all, outer_full, preferred_element_type=jnp.float32)
    unused_act, act_back = jax.vjp(gated_act, gates)
    gates_grad = act_back(hidden_grad)[0].astype(jnp.bfloat16)
    inner_grad = jnp.einsum(
        "ld,lcf->dcf", inner_all, gates_grad, preferred_element_type=jnp.float32
    )
    piece_rows = gates_grad
    inner_in_grad = lax.psum_scatter(
        jnp.einsum("lcf,dcf->ld", piece_rows, inner_full, preferred_element_type=jnp.float32),
        "mp",
        scatter_dimension=0,
        tiled=True,
    )
    unused_norm, mlp_norm_back = jax.vjp(layer_norm, middle, mlp_gain)
    middle_norm_grad, mlp_gain_part = mlp_norm_back(inner_in_grad)
    middle_grad = grad_out.astype(jnp.float32) + middle_norm_grad
    middle_low = middle_grad.astype(jnp.bfloat16)
    middle_all = lax.all_gather(middle_low, "mp", axis=0, tiled=True)
    attn_grad = lax.dot_general(
        middle_all, heads_out, (((0,), (0,)), ((), ())), preferred_element_type=jnp.float32
    )
    heads_grad = (
        jnp.dot(middle_all, attn_full, preferred_element_type=jnp.float32)
        .astype(jnp.bfloat16)
        .reshape(head_shape)
    )

    def backward_block(partials, block_index):
        key_acc, value_acc = partials
        row_start = block_index * block_rows
        allowed, live_rows = block_masks(segment, row_start, block_rows)
        q_rows = lax.dynamic_slice_in_dim(query_rot, row_start, block_rows)
        grad_rows = lax.dynamic_slice_in_dim(heads_grad, row_start, block_rows)
        masked = masked_scores(q_rows, key_rot, allowed, score_scale)
        attn_prob = (
            jnp.exp(masked - row_tops[block_index][..., None]) / row_totals[block_index][..., None]
        )
        prob_grad = jnp.einsum(
            "qhe,khe->hqk", grad_rows, value_rows, preferred_element_type=jnp.float32
        )
        row_dots = jnp.sum(attn_prob * prob_grad, axis=-1, keepdims=True)
        score_grad = (attn_prob * (prob_grad - row_dots)).astype(jnp.bfloat16)
        query_part = (
            jnp.einsum("hqk,khe->qhe", score_grad, key_rot, preferred_element_type=jnp.float32)
            * score_scale
        )
        key_acc = (
            key_acc
            + jnp.einsum("hqk,qhe->khe", score_grad, q_rows, preferred_element_type=jnp.float32)
            * score_scale
        )
        value_acc = value_acc + jnp.einsum(
            "hqk,qhe->khe",
            attn_prob.astype(jnp.bfloat16),
            grad_rows,
            preferred_element_type=jnp.float32,
        )
        return ((key_acc, value_acc), query_part)

    zero_heads = jnp.zeros(head_shape, jnp.float32)
    (key_grad, value_grad), query_parts = lax.scan(
        backward_block, (zero_heads, zero_heads), block_ids
    )
    query_grad = query_parts.reshape(head_shape)

    def turn_heads(values):
        return rotary(values, angle)

    unused_turn, turn_back = jax.vjp(turn_heads, zero_heads)
    query_raw = turn_back(query_grad)[0].reshape(seq_length, head_cols)
    key_raw = turn_back(key_grad)[0].reshape(seq_length, head_cols)
    qkv_low = jnp.stack(
        [query_raw, key_raw, value_grad.reshape(seq_length, head_cols)], axis=1
    ).astype(jnp.bfloat16)
    qkv_grad = jnp.einsum("ld,lcf->dcf", normed_all, qkv_low, preferred_element_type=jnp.float32)
    piece_rows = qkv_low
    normed_grad = lax.psum_scatter(
        jnp.einsum("lcf,dcf->ld", piece_rows, qkv_full, preferred_element_type=jnp.float32).astype(
            jnp.bfloat16
        ),
        "mp",
        scatter_dimension=0,
        tiled=True,
    ).astype(jnp.float32)
    unused_first, attn_norm_back = jax.vjp(layer_norm, tokens, attn_gain)
    tokens_norm_grad, attn_gain_part = attn_norm_back(normed_grad)
    input_grad = middle_grad + tokens_norm_grad
    qkv_sum, attn_sum, inner_sum, outer_sum = (
        lax.psum_scatter(qkv_grad, "dp", scatter_dimension=0, tiled=True),
        lax.psum_scatter(attn_grad, "dp", scatter_dimension=0, tiled=True),
        lax.psum_scatter(inner_grad, "dp", scatter_dimension=0, tiled=True),
        lax.psum_scatter(outer_grad, "dp", scatter_dimension=0, tiled=True),
    )
    square_sums, live_total, attn_gain_grad, mlp_gain_grad = lax.psum(
        (squares, live_count, attn_gain_part, mlp_gain_part), ("dp", "mp")
    )
    rms_values = jnp.sqrt(square_sums / (live_total * feature_count))
    return (
        layer_output,
        input_grad,
        qkv_sum,
        attn_sum,
        inner_sum,
        outer_sum,
        attn_gain_grad,
        mlp_gain_grad,
        rms_values,
    )


def solution(mesh):
    return jax.shard_map(
        local,
        mesh=mesh,
        in_specs=(
            P(("dp", "mp"), None),
            P("dp", None),
            P(("dp", "mp"), None),
            P("dp", None, "mp"),
            P("dp", "mp"),
            P("dp", None, "mp"),
            P("dp", "mp"),
            P(),
            P(),
        ),
        out_specs=(
            P(("dp", "mp"), None),
            P(("dp", "mp"), None),
            P("dp", None, "mp"),
            P("dp", "mp"),
            P("dp", None, "mp"),
            P("dp", "mp"),
            P(),
            P(),
            P(),
        ),
        check_vma=False,
    )
```

profile of v0, /device:TPU:0, one launch (start us, length us, event | category | flops | bytes accessed | tf_op | source)
XLA Modules:
  0.0 1491.7 jit_solution(2605310749353650712)
XLA Ops:
  15.5 13.0 all_gather.26
  40.1 82.9 %all-gather.8.cloned.1.call-done = bf16[2048,1024]{1,0:T(8,128)(2,1)} async-done(((bf16[512,1024]{1,0:T(8,128)(2,1)}), bf16[2048,1024]{1,0:T(8,128)(2,1)}) %all-gather.8.cloned.1.call-update) | async-done | bytes 4194320 | tf_op jit(solution)/shard_map/all_gather | solution.py:103
  130.4 62.6 %while.29 = (s32[]{:T(128)}, bf16[4,512,4,64]{1,3,2,0:T(8,128)(2,1)}, f32[4,4,512]{2,1,0:T(4,128)S(1)}, f32[4,4,512]{2,1,0:T(4,128)S(1)}, s32[4]{0:T(128)S(1)}, ...) while((s32[]{:T(128)}, ...), condition=%wide.region_7.8_spmd, body=%wide.region_4.7_spmd.sunk | while | flops 1126306304 | bytes 57271000 | solution.py:124
  203.7 141.1 %reduce-scatter.9.cloned.1.call-done = f32[512,1024]{1,0:T(8,128)} async-done(((f32[2048,1024]{1,0:T(8,128)}), f32[512,1024]{1,0:T(8,128)}) %reduce-scatter.9.cloned.1.call-update) | async-done | bytes 2097168 | tf_op jit(solution)/shard_map/reduce_scatter | solution.py:127
  348.7 23.5 %all-gather.16.cloned.1.call-done = bf16[1024,656]{0,1:T(8,128)(2,1)} async-done(((bf16[128,656]{0,1:T(8,128)(2,1)}), bf16[1024,656]{0,1:T(8,128)(2,1)}) %all-gather.16.cloned.1.call-update) | async-done | bytes 1343504 | tf_op jit(solution)/shard_map/all_gather | solution.py:138
  372.2 82.2 %all-gather.18.cloned.1.call-done = bf16[2048,1024]{1,0:T(8,128)(2,1)} async-done(((bf16[512,1024]{1,0:T(8,128)(2,1)}), bf16[2048,1024]{1,0:T(8,128)(2,1)}) %all-gather.18.cloned.1.call-update) | async-done | bytes 4194320 | tf_op jit(solution)/shard_map/all_gather | solution.py:163
  462.3 23.2 %all-gather.14.cloned.1.call-done = bf16[1024,2,656]{0,2,1:T(8,128)(2,1)} async-done(((bf16[128,2,656]{0,2,1:T(8,128)(2,1)}), bf16[1024,2,656]{0,2,1:T(8,128)(2,1)}) %all-gather.14.cloned.1.call-update) | async-done | bytes 2686992 | tf_op jit(solution)/shard_map/all_gather | solution.py:137
  485.5 82.9 %all-gather.12.cloned.1.call-done = bf16[2048,1024]{1,0:T(8,128)(2,1)} async-done(((bf16[512,1024]{1,0:T(8,128)(2,1)}), bf16[2048,1024]{1,0:T(8,128)(2,1)}) %all-gather.12.cloned.1.call-update) | async-done | bytes 4194320 | tf_op jit(solution)/shard_map/all_gather | solution.py:141
  577.0 12.5 multiply_bitcast_fusion
  594.7 13.5 convolution_bitcast_fusion
  617.0 134.4 %reduce-scatter.13.cloned.1.call-done = f32[512,1024]{1,0:T(8,128)} async-done(((f32[2048,1024]{1,0:T(8,128)}), f32[512,1024]{1,0:T(8,128)}) %reduce-scatter.13.cloned.1.call-update) | async-done | bytes 2097168 | tf_op jit(solution)/shard_map/reduce_scatter | solution.py:174
  754.7 76.5 %reduce-scatter.11.cloned.1.call-done = bf16[512,1024]{1,0:T(8,128)(2,1)} async-done(((bf16[2048,1024]{1,0:T(8,128)(2,1)}), bf16[512,1024]{1,0:T(8,128)(2,1)}) %reduce-scatter.11.cloned.1.call-update) | async-done | bytes 1048592 | tf_op jit(solution)/shard_map/reduce_scatter | solution.py:145
  839.0 81.3 %all-gather.20.cloned.1.call-done = bf16[2048,1024]{1,0:T(8,128)(2,1)} async-done(((bf16[512,1024]{1,0:T(8,128)(2,1)}), bf16[2048,1024]{1,0:T(8,128)(2,1)}) %all-gather.20.cloned.1.call-update) | async-done | bytes 4194320 | tf_op jit(solution)/shard_map/all_gather | solution.py:184
  924.9 263.5 %while.30 = (s32[]{:T(128)}, f32[2048,4,64]{0,2,1:T(8,128)S(1)}, f32[2048,4,64]{0,2,1:T(8,128)}, f32[4,512,4,64]{1,0,3,2:T(4,128)}, s32[4]{0:T(128)S(1)}, /*inde...) while((s32[]{:T(128)}, f32[2048,4,64]{0,2,1:T(8,128)S(1)}, ...), condition=%wide.region_17.18_spmd.clone, body=%wide.region_15.17_spmd.clone.sunk | while | flops 2731145728 | bytes 147406160 | solution.py:227
  938.6 14.7 multiply_reduce_fusion.5
  953.4 11.3 multiply_convert_fusion.4
  979.3 11.1 dynamic_update_slice.24
  1004.0 14.8 multiply_reduce_fusion.5
  1018.8 11.3 multiply_convert_fusion.4
  1045.3 11.1 dynamic_update_slice.24
  1070.0 14.7 multiply_reduce_fusion.5
  1084.7 11.3 multiply_convert_fusion.4
  1111.3 11.1 dynamic_update_slice.24
  1136.0 14.8 multiply_reduce_fusion.5
  1150.7 11.3 multiply_convert_fusion.4
  1177.2 11.1 dynamic_update_slice.24
  1216.5 11.2 fusion.53
  1241.6 42.7 %reduce-scatter.15.cloned.1.call-done = bf16[512,1024]{1,0:T(8,128)(2,1)} async-done(((bf16[2048,1024]{1,0:T(8,128)(2,1)}), bf16[512,1024]{1,0:T(8,128)(2,1)}) %reduce-scatter.15.cloned.1.call-update) | async-done | bytes 1048592 | tf_op jit(solution)/shard_map/reduce_scatter | solution.py:243
  1292.0 41.0 %all-reduce.6 = (f32[1024]{0:T(1024)}, f32[1024]{0:T(1024)}, f32[4]{0:T(128)S(1)}, f32[]{:T(128)}) all-reduce(f32[1024]{0:T(1024)S(1)} %get-tuple-element.182, f32[1024]{0:T(1024)S(1)} %copy-done.31, f32[4]{0:T(128)S(1)} %pad_maximum_fusion.5, f32[]{:T(128)} %get-tuple-element.242), channel_id=1, replica_groups=mesh['dp'=8,'mp'=4] {'dp','mp'}, use_global_device_ids=true, to_apply=%region_26.27 | all-reduce | flops 2053 | bytes 16424 | tf_op jit(solution)/shard_map/psum | solution.py:260
  1338.1 57.1 %reduce-scatter.21.cloned.1.call-done = f32[128,2,656]{0,2,1:T(8,128)} async-done(((f32[1024,2,656]{0,2,1:T(8,128)}), f32[128,2,656]{0,2,1:T(8,128)}) %reduce-scatter.21.cloned.1.call-update) | async-done | bytes 671760 | tf_op jit(solution)/shard_map/reduce_scatter | solution.py:257
  1395.2 39.6 %reduce-scatter.19.cloned.1.call-done = f32[128,256]{1,0:T(8,128)} async-done(((f32[1024,256]{1,0:T(8,128)}), f32[128,256]{1,0:T(8,128)}) %reduce-scatter.19.cloned.1.call-update) | async-done | bytes 131088 | tf_op jit(solution)/shard_map/reduce_scatter | solution.py:256
  1434.8 50.1 %reduce-scatter.17.cloned.1.call-done = f32[128,3,256]{2,0,1:T(8,128)} async-done(((f32[1024,3,256]{2,0,1:T(8,128)}), f32[128,3,256]{2,0,1:T(8,128)}) %reduce-scatter.17.cloned.1.call-update) | async-done | bytes 393232 | tf_op jit(solution)/shard_map/reduce_scatter | solution.py:255
  (239 shorter events, 305.2 us)
Async XLA Ops:
  7.2 32.9 %all-gather.10.cloned.1.call-start = ((), (), s32[]{:S(2)}) async-start(), calls=%async_computation.9 | async-start | bytes 1769472 | tf_op jit(solution)/shard_map/all_gather | solution.py:99
  9.0 114.0 %all-gather.8.cloned.1.call-start = ((), (), s32[]{:S(2)}) async-start(), calls=%async_computation.8 | async-start | bytes 5242880 | tf_op jit(solution)/shard_map/all_gather | solution.py:103
  14.8 330.1 %reduce-scatter.9.cloned.1.call-start = ((), (), s32[]{:S(2)}) async-start(), calls=%async_computation.10 | async-start | bytes 10485760 | tf_op jit(solution)/shard_map/reduce_scatter | solution.py:127
  29.5 100.0 %copy-start.11 = (f32[2048,32]{0,1:T(8,128)}, f32[2048,32]{0,1:T(8,128)S(1)}, u32[]{:S(2)}) copy-start(f32[2048,32]{0,1:T(8,128)S(1)} %get-tuple-element.277) | copy-start | bytes 786436
  29.6 100.0 %copy-start.13 = (f32[2048,32]{0,1:T(8,128)}, f32[2048,32]{0,1:T(8,128)S(1)}, u32[]{:S(2)}) copy-start(f32[2048,32]{0,1:T(8,128)S(1)} %get-tuple-element.278) | copy-start | bytes 786436
  201.7 170.5 %all-gather.16.cloned.1.call-start = ((), (), s32[]{:S(2)}) async-start(), calls=%async_computation.13 | async-start | bytes 1511424 | tf_op jit(solution)/shard_map/all_gather | solution.py:138
  202.3 145.1 %copy-start.22 = (f32[1024]{0:T(1024)S(1)}, f32[1024]{0:T(1024)}, u32[]{:S(2)}) copy-start(f32[1024]{0:T(1024)} %param.21) | copy-start | bytes 12292
  202.3 252.1 %all-gather.18.cloned.1.call-start = ((), (), s32[]{:S(2)}) async-start(), calls=%async_computation.15 | async-start | bytes 5242880 | tf_op jit(solution)/shard_map/all_gather | solution.py:163
  202.9 282.6 %all-gather.14.cloned.1.call-start = ((), (), s32[]{:S(2)}) async-start(), calls=%async_computation.12 | async-start | bytes 3022848 | tf_op jit(solution)/shard_map/all_gather | solution.py:137
  203.4 365.0 %all-gather.12.cloned.1.call-start = ((), (), s32[]{:S(2)}) async-start(), calls=%async_computation.11 | async-start | bytes 5242880 | tf_op jit(solution)/shard_map/all_gather | solution.py:141
  348.7 402.7 %reduce-scatter.13.cloned.1.call-start = ((), (), s32[]{:S(2)}) async-start(), calls=%async_computation.16 | async-start | bytes 10485760 | tf_op jit(solution)/shard_map/reduce_scatter | solution.py:174
  608.2 223.0 %reduce-scatter.11.cloned.1.call-start = ((), (), s32[]{:S(2)}) async-start(), calls=%async_computation.14 | async-start | bytes 5242880 | tf_op jit(solution)/shard_map/reduce_scatter | solution.py:145
  616.3 304.0 %all-gather.20.cloned.1.call-start = ((), (), s32[]{:S(2)}) async-start(), calls=%async_computation.17 | async-start | bytes 5242880 | tf_op jit(solution)/shard_map/all_gather | solution.py:184
  617.0 219.3 %copy-start.23 = (f32[1,512]{1,0:T(1,128)}, f32[1,512]{1,0:T(1,128)S(1)}, u32[]{:S(2)}) copy-start(f32[1,512]{1,0:T(1,128)S(1)} %get-tuple-element.243) | copy-start | bytes 6148
  838.9 445.5 %reduce-scatter.15.cloned.1.call-start = ((), (), s32[]{:S(2)}) async-start(), calls=%async_computation.18 | async-start | bytes 5242880 | tf_op jit(solution)/shard_map/reduce_scatter | solution.py:243
  929.1 9.5 copy-start.6
  994.5 9.5 copy-start.6
  1060.5 9.5 copy-start.6
  1126.4 9.5 copy-start.6
  1208.9 129.1 %reduce-scatter.23.cloned.1.call-start = ((), (), s32[]{:S(2)}) async-start(), calls=%async_computation.22 | async-start | bytes 3022848 | tf_op jit(solution)/shard_map/reduce_scatter | solution.py:258
  1216.5 178.7 %reduce-scatter.21.cloned.1.call-start = ((), (), s32[]{:S(2)}) async-start(), calls=%async_computation.21 | async-start | bytes 6045696 | tf_op jit(solution)/shard_map/reduce_scatter | solution.py:257
  1227.8 207.0 %reduce-scatter.19.cloned.1.call-start = ((), (), s32[]{:S(2)}) async-start(), calls=%async_computation.20 | async-start | bytes 1179648 | tf_op jit(solution)/shard_map/reduce_scatter | solution.py:256
  1233.5 50.9 %copy-start = (bf16[512,1024]{1,0:T(8,128)(2,1)S(1)}, bf16[512,1024]{1,0:T(8,128)(2,1)}, u32[]{:S(2)}) copy-start(bf16[512,1024]{1,0:T(8,128)(2,1)} %param.13) | copy-start | bytes 3145732
  1233.5 50.8 %copy-start.19 = (f32[512]{0:T(512)S(1)}, f32[512]{0:T(512)}, u32[]{:S(2)}) copy-start(f32[512]{0:T(512)} %copy-done.18) | copy-start | bytes 6148
  1233.5 50.8 %copy-start.20 = (f32[1024]{0:T(1024)S(1)}, f32[1024]{0:T(1024)}, u32[]{:S(2)}) copy-start(f32[1024]{0:T(1024)} %param.20) | copy-start | bytes 12292
  1233.6 251.3 %reduce-scatter.17.cloned.1.call-start = ((), (), s32[]{:S(2)}) async-start(), calls=%async_computation.19 | async-start | bytes 3538944 | tf_op jit(solution)/shard_map/reduce_scatter | solution.py:255
  1241.6 44.6 %copy-start.30 = (f32[512]{0:T(512)S(1)}, f32[512]{0:T(512)}, u32[]{:S(2)}) copy-start(f32[512]{0:T(512)} %copy-done.29) | copy-start | bytes 6148
  1241.6 44.6 %copy-start.24 = (f32[1,512]{1,0:T(1,128)S(1)}, f32[1,512]{1,0:T(1,128)}, u32[]{:S(2)}) copy-start(f32[1,512]{1,0:T(1,128)} %copy-done.23) | copy-start | bytes 6148
  1241.6 44.6 %copy-start.26 = (f32[512]{0:T(512)S(1)}, f32[512]{0:T(512)}, u32[]{:S(2)}) copy-start(f32[512]{0:T(512)} %copy-done.25) | copy-start | bytes 6148
  1241.6 50.5 %copy-start.31 = (f32[1024]{0:T(1024)S(1)}, f32[1024]{0:T(1024)}, u32[]{:S(2)}) copy-start(f32[1024]{0:T(1024)} %get-tuple-element.180) | copy-start | bytes 12292
  1241.6 92.7 %copy-start.4 = (f32[512,1024]{1,0:T(8,128)S(1)}, f32[512,1024]{1,0:T(8,128)}, u32[]{:S(2)}) copy-start(f32[512,1024]{1,0:T(8,128)} %copy-done.3) | copy-start | bytes 6291460
  1241.6 92.7 %copy-start.28 = (f32[512]{0:T(512)S(1)}, f32[512]{0:T(512)}, u32[]{:S(2)}) copy-start(f32[512]{0:T(512)} %copy-done.27) | copy-start | bytes 6148
  (18 other events, 80.0 us)
Sparse Core Ops, SparseCore 0:
  10.5 29.5 all-gather.9
  42.2 80.7 all-gather.7
  201.8 142.9 reduce-scatter.8
  346.6 25.5 all-gather.15
  373.6 80.7 all-gather.17
  456.1 29.3 all-gather.13
  487.6 80.7 all-gather.11
  608.4 142.9 reduce-scatter.12
  753.7 77.4 reduce-scatter.10
  839.0 81.2 all-gather.19
  1209.1 75.2 reduce-scatter.14
  1288.2 45.6 reduce-scatter.22
  1338.0 57.1 reduce-scatter.20
  1398.8 35.9 reduce-scatter.18
  1438.6 46.2 reduce-scatter.16
where the time goes:
time: 1500 us; the launch traced here: 1490 us
  waiting for transfers between devices  930 us (62%)
  matrix products  279 us (19%)
  other arithmetic  127 us (8%)
  local copies, waits for them, and re-layouts  71.7 us (5%)
  blocking collectives  54 us (4%)
  between operations  15.3 us (1%)
    reduce_scatter x1, waiting for transfers between devices, local(): lax.psum_scatter(lax.dot_general(piece_rows, attn_full, (((1,), (1,)), ((...  141 us
    reduce_scatter x1, waiting for transfers between devices, local(): lax.psum_scatter(jnp.einsum('lcf,dcf->ld', piece_rows, inner_full, prefer...  134 us
    all_gather x1, waiting for transfers between devices, local(): normed_all = lax.all_gather(normed, 'mp', axis=0, tiled=True)  82.9 us
    all_gather x1, waiting for transfers between devices, local(): inner_all = lax.all_gather(inner_in, 'mp', axis=0, tiled=True)  82.9 us
    all_gather x1, waiting for transfers between devices, local(): grad_all = lax.all_gather(grad_out, 'mp', axis=0, tiled=True)  82.2 us
    all_gather x1, waiting for transfers between devices, local(): middle_all = lax.all_gather(middle_low, 'mp', axis=0, tiled=True)  81.3 us
    reduce_scatter x1, waiting for transfers between devices, local(): lax.psum_scatter(lax.dot_general(piece_rows, outer_full, (((1,), (1,)), (...  76.5 us
    dot_general x8, matrix products, masked_scores(): jnp.einsum('qhe,khe->hqk', q_rows, key_rot, preferred_element_type=jnp.fl...  71.9 us
  transfers between devices with their start and end apart: 15, of which 14 were waited for; matrix products, arithmetic and copies ran while one was open for 5% of the time, Pallas kernels for 0%

commit v1 on v0

v1 whole, which is shorter than its diff:
```python
import functools
import math

import jax
import jax.numpy as jnp
from jax import lax
from jax.experimental import pallas as pl
from jax.experimental.pallas import tpu as pltpu
from jax.sharding import PartitionSpec as P

HEAD_DIM = 64
NORM_EPS = 1e-05
ROPE_BASE = 160000.0
BIG = 1e30
LANES = 128
BF = jnp.bfloat16
F32 = jnp.float32
VMEM_LIMIT = 60 * 1024 * 1024


def dot_nn(a, b):
    return lax.dot_general(a, b, (((1,), (0,)), ((), ())), preferred_element_type=F32)


def dot_nt(a, b):
    return lax.dot_general(a, b, (((1,), (1,)), ((), ())), preferred_element_type=F32)


def dot_tn(a, b):
    return lax.dot_general(a, b, (((0,), (0,)), ((), ())), preferred_element_type=F32)


def norm_stats(values):
    centre = jnp.mean(values, axis=-1, keepdims=True)
    shifted = values - centre
    spread = jnp.mean(shifted * shifted, axis=-1, keepdims=True)
    scale = lax.rsqrt(spread + NORM_EPS)
    return shifted * scale, scale


def norm_back(vhat, scale, gain, grad):
    u = grad * gain
    mean_u = jnp.mean(u, axis=-1, keepdims=True)
    mean_uv = jnp.mean(u * vhat, axis=-1, keepdims=True)
    return scale * (u - mean_u - vhat * mean_uv)


def doc_positions(segment):
    length = segment.shape[0]
    places = jnp.arange(length, dtype=jnp.int32)
    before = jnp.concatenate([jnp.full((1,), -1, jnp.int32), segment[:-1]])
    starts = jnp.where(segment != before, places, jnp.zeros_like(places))
    return places - lax.cummax(starts, axis=0)


def rope_tables(segment):
    half = HEAD_DIM // 2
    lane = jnp.arange(LANES, dtype=jnp.int32)
    frequency = jnp.exp(
        (lane % half).astype(F32) * (-2.0 * math.log(ROPE_BASE) / HEAD_DIM)
    )
    angle = doc_positions(segment).astype(F32)[:, None] * frequency[None, :]
    first = (lane % HEAD_DIM < half)[None, :]
    sine = jnp.sin(angle)
    return jnp.cos(angle), jnp.where(first, -sine, sine)


def swap_halves(values):
    lane = lax.broadcasted_iota(jnp.int32, values.shape, 1)
    first = lane % HEAD_DIM < HEAD_DIM // 2
    back = pltpu.roll(values, LANES - HEAD_DIM // 2, 1)
    ahead = pltpu.roll(values, HEAD_DIM // 2, 1)
    return jnp.where(first, back, ahead)


def qkv_kernel(x_ref, gain_ref, w_ref, cos_ref, sin_ref, n_ref, q_ref, k_ref, v_ref):
    vhat, unused = norm_stats(x_ref[...].astype(F32))
    normed = (vhat * gain_ref[...]).astype(BF)
    n_ref[...] = normed
    cols = q_ref.shape[1]
    flat = dot_nn(normed, w_ref[...])
    cosine = cos_ref[...]
    sine = sin_ref[...]
    for part, out in ((0, q_ref), (1, k_ref)):
        for at in range(0, cols, LANES):
            u = flat[:, part * cols + at : part * cols + at + LANES]
            out[:, at : at + LANES] = (u * cosine + swap_halves(u) * sine).astype(BF)
    v_ref[...] = flat[:, 2 * cols :].astype(BF)


def qkv_call(x_all, gain, weight, cosine, sine):
    tokens, model = x_all.shape
    cols = weight.shape[1] // 3
    rows = 512
    whole = lambda i: (0, 0)
    block = lambda i: (i, 0)
    return pl.pallas_call(
        qkv_kernel,
        grid=(tokens // rows,),
        in_specs=[
            pl.BlockSpec((rows, model), block),
            pl.BlockSpec((1, model), whole),
            pl.BlockSpec(weight.shape, whole),
            pl.BlockSpec((rows, LANES), block),
            pl.BlockSpec((rows, LANES), block),
        ],
        out_specs=[
            pl.BlockSpec((rows, model), block),
            pl.BlockSpec((rows, cols), block),
            pl.BlockSpec((rows, cols), block),
            pl.BlockSpec((rows, cols), block),
        ],
        out_shape=[
            jax.ShapeDtypeStruct((tokens, model), BF),
            jax.ShapeDtypeStruct((tokens, cols), BF),
            jax.ShapeDtypeStruct((tokens, cols), BF),
            jax.ShapeDtypeStruct((tokens, cols), BF),
        ],
        compiler_params=pltpu.CompilerParams(vmem_limit_bytes=VMEM_LIMIT),
        cost_estimate=pl.CostEstimate(
            flops=2 * tokens * model * 3 * cols, bytes_accessed=16 << 20, transcendentals=0
        ),
        name="qkv",
    )(x_all, gain, weight, cosine, sine)


def attn_fwd_kernel(q_ref, k_ref, v_ref, qaux_ref, kaux_ref, live_ref, o_ref, qa_ref, ka_ref, s_ref):
    step = pl.program_id(0)
    keys = k_ref.shape[0]
    rows = q_ref.shape[0]
    chunk = 512
    lane_k = lax.broadcasted_iota(jnp.int32, (keys, LANES), 1)
    lane = lax.broadcasted_iota(jnp.int32, (rows, LANES), 1)

    @pl.when(step == 0)
    def _():
        k = k_ref[...]
        kaux = kaux_ref[...]
        ka_ref[0] = jnp.where(lane_k < HEAD_DIM, k, kaux)
        ka_ref[1] = jnp.where(lane_k >= HEAD_DIM, k, kaux)

    q = q_ref[...] * jnp.asarray(HEAD_DIM**-0.5, BF)
    qaux = qaux_ref[...]
    live = live_ref[...]
    outs = []
    for head in range(2):
        mine = (lane < HEAD_DIM) if head == 0 else (lane >= HEAD_DIM)
        qa = jnp.where(mine, q, qaux)
        top = None
        for at in range(0, keys, chunk):
            s = dot_nt(qa, ka_ref[head, at : at + chunk, :])
            s_ref[:, at : at + chunk] = s
            part = jnp.max(s, axis=-1, keepdims=True)
            top = part if top is None else jnp.maximum(top, part)
        total = jnp.zeros((rows, 1), F32)
        mixed = jnp.zeros((rows, LANES), F32)
        for at in range(0, keys, chunk):
            p = jnp.exp(s_ref[:, at : at + chunk] - top)
            total += jnp.sum(p, axis=-1, keepdims=True)
            mixed += dot_nn(p.astype(BF), v_ref[at : at + chunk, :])
        outs.append(mixed * (live / total))
        log_sum = jnp.where(live > 0, top + jnp.log(total), BIG)
        high = log_sum.astype(BF)
        rest = log_sum - high.astype(F32)
        mid = rest.astype(BF)
        low = (rest - mid.astype(F32)).astype(BF)
        t = lane % HEAD_DIM
        aux = jnp.where(t == 16, -high, jnp.where(t == 17, -mid, jnp.where(t == 18, -low, qaux)))
        qa_ref[head] = jnp.where(mine, q, aux)
    o_ref[...] = jnp.where(lane < HEAD_DIM, outs[0], outs[1]).astype(BF)


def attn_fwd_call(q, k, v, qaux, kaux, live, pair):
    tokens = q.shape[0]
    rows = 256
    whole = lambda i: (0, 0)
    block = lambda i: (i, 0)
    return pl.pallas_call(
        attn_fwd_kernel,
        grid=(tokens // rows,),
        in_specs=[
            pl.BlockSpec((rows, LANES), lambda i: (i, pair)),
            pl.BlockSpec((tokens, LANES), lambda i: (0, pair)),
            pl.BlockSpec((tokens, LANES), lambda i: (0, pair)),
            pl.BlockSpec((rows, LANES), block),
            pl.BlockSpec((tokens, LANES), whole),
            pl.BlockSpec((rows, 1), block),
        ],
        out_specs=[
            pl.BlockSpec((rows, LANES), block),
            pl.BlockSpec((2, rows, LANES), lambda i: (0, i, 0)),
            pl.BlockSpec((2, tokens, LANES), lambda i: (0, 0, 0)),
        ],
        out_shape=[
            jax.ShapeDtypeStruct((tokens, LANES), BF),
            jax.ShapeDtypeStruct((2, tokens, LANES), BF),
            jax.ShapeDtypeStruct((2, tokens, LANES), BF),
        ],
        scratch_shapes=[pltpu.VMEM((rows, tokens), F32)],
        compiler_params=pltpu.CompilerParams(vmem_limit_bytes=VMEM_LIMIT),
        cost_estimate=pl.CostEstimate(
            flops=8 * tokens * tokens * LANES, bytes_accessed=4 << 20, transcendentals=0
        ),
        name="attn_fwd",
    )(q, k, v, qaux, kaux, live)


def attn_bwd_kernel(
    qa_ref, ka_ref, v_ref, do_ref, o_ref, cosq_ref, sinq_ref, cosk_ref, sink_ref,
    dq_ref, dk_ref, dv_ref, va_ref, kt_ref, dk_acc, dv_acc,
):
    step = pl.program_id(0)
    keys = v_ref.shape[0]
    rows = do_ref.shape[0]
    chunk = 512
    lane_k = lax.broadcasted_iota(jnp.int32, (keys, LANES), 1)
    lane = lax.broadcasted_iota(jnp.int32, (rows, LANES), 1)
    zero = jnp.zeros((), BF)

    @pl.when(step == 0)
    def _():
        v = v_ref[...]
        ones = jnp.where(lane_k % HEAD_DIM < 3, jnp.ones((), BF), zero)
        for head in range(2):
            mine = (lane_k < HEAD_DIM) if head == 0 else (lane_k >= HEAD_DIM)
            va_ref[head] = jnp.where(mine, v, ones)
            own = jnp.where(mine, ka_ref[head], zero).astype(F32)
            kt_ref[head] = own.T.astype(BF)
        dk_acc[...] = jnp.zeros_like(dk_acc)
        dv_acc[...] = jnp.zeros_like(dv_acc)

    grad = do_ref[...]
    product = grad.astype(F32) * o_ref[...].astype(F32)
    turned = jnp.zeros((LANES, rows), F32)
    for head in range(2):
        mine = (lane < HEAD_DIM) if head == 0 else (lane >= HEAD_DIM)
        delta = jnp.sum(jnp.where(mine, product, 0.0), axis=-1, keepdims=True)
        high = delta.astype(BF)
        rest = delta - high.astype(F32)
        mid = rest.astype(BF)
        low = (rest - mid.astype(F32)).astype(BF)
        t = lane % HEAD_DIM
        aux = jnp.where(t == 0, -high, jnp.where(t == 1, -mid, jnp.where(t == 2, -low, zero)))
        grad_aug = jnp.where(mine, grad, aux)
        grad_own = jnp.where(mine, grad, zero)
        qa = qa_ref[head]
        q_own = jnp.where(mine, qa, zero)
        for at in range(0, keys, chunk):
            some = slice(at, at + chunk)
            prob = jnp.exp(dot_nt(ka_ref[head, some, :], qa))
            back = dot_nt(va_ref[head, some, :], grad_aug)
            score_grad = (prob * back).astype(BF)
            dv_acc[some, :] += dot_nn(prob.astype(BF), grad_own)
            dk_acc[some, :] += dot_nn(score_grad, q_own)
            turned += dot_nn(kt_ref[head, :, some], score_grad)
    dq = turned.T * (HEAD_DIM**-0.5)
    dq_ref[...] = (dq * cosq_ref[...] - swap_halves(dq) * sinq_ref[...]).astype(BF)

    @pl.when(step == pl.num_programs(0) - 1)
    def _():
        dk = dk_acc[...]
        dk_ref[...] = (dk * cosk_ref[...] - swap_halves(dk) * sink_ref[...]).astype(BF)
        dv_ref[...] = dv_acc[...].astype(BF)


def attn_bwd_call(qa, ka, v, grad, o, cosine, sine, pair):
    tokens = v.shape[0]
    rows = 256
    whole = lambda i: (0, 0)
    block = lambda i: (i, 0)
    return pl.pallas_call(
        attn_bwd_kernel,
        grid=(tokens // rows,),
        in_specs=[
            pl.BlockSpec((2, rows, LANES), lambda i: (0, i, 0)),
            pl.BlockSpec((2, tokens, LANES), lambda i: (0, 0, 0)),
            pl.BlockSpec((tokens, LANES), lambda i: (0, pair)),
            pl.BlockSpec((rows, LANES), block),
            pl.BlockSpec((rows, LANES), block),
            pl.BlockSpec((rows, LANES), block),
            pl.BlockSpec((rows, LANES), block),
            pl.BlockSpec((tokens, LANES), whole),
            pl.BlockSpec((tokens, LANES), whole),
        ],
        out_specs=[
            pl.BlockSpec((rows, LANES), block),
            pl.BlockSpec((tokens, LANES), whole),
            pl.BlockSpec((tokens, LANES), whole),
        ],
        out_shape=[jax.ShapeDtypeStruct((tokens, LANES), BF)] * 3,
        scratch_shapes=[
            pltpu.VMEM((2, tokens, LANES), BF),
            pltpu.VMEM((2, LANES, tokens), BF),
            pltpu.VMEM((tokens, LANES), F32),
            pltpu.VMEM((tokens, LANES), F32),
        ],
        compiler_params=pltpu.CompilerParams(vmem_limit_bytes=VMEM_LIMIT),
        cost_estimate=pl.CostEstimate(
            flops=20 * tokens * tokens * LANES, bytes_accessed=6 << 20, transcendentals=0
        ),
        name="attn_bwd",
    )(qa, ka, v, grad, o, cosine, sine, cosine, sine)


def ffn_kernel(x_ref, g_ref, w_ref, mlp_ref, back_ref, dw_ref):
    step = pl.program_id(0)
    blocks = w_ref.shape[0]

    def weight(part):
        return jnp.concatenate([w_ref[d, 0, part] for d in range(blocks)], axis=-1)

    x = x_ref[...]
    grad = g_ref[...]
    w_act, w_lin, w_out = weight(0), weight(1), weight(2)
    act_in = dot_nt(w_act, x)
    linear = dot_nt(w_lin, x)
    hidden_grad = dot_nt(w_out, grad)
    cdf = 0.5 * (1.0 + lax.erf(act_in * (2.0**-0.5)))
    act = act_in * cdf
    slope = cdf + act_in * jnp.exp(-0.5 * act_in * act_in) * ((2.0 * math.pi) ** -0.5)
    hidden = (act * linear).astype(BF)
    d_act = (hidden_grad * linear * slope).astype(BF)
    d_lin = (hidden_grad * act).astype(BF)

    def put(part, value):
        value = value.astype(BF)
        for d in range(blocks):
            dw_ref[d, 0, part] = value[:, d * LANES : (d + 1) * LANES]

    put(2, dot_nn(hidden, grad))
    put(0, dot_nn(d_act, x))
    put(1, dot_nn(d_lin, x))
    mlp = dot_tn(hidden, w_out)
    back = dot_tn(d_act, w_act) + dot_tn(d_lin, w_lin)

    @pl.when(step == 0)
    def _():
        mlp_ref[...] = mlp
        back_ref[...] = back

    @pl.when(step > 0)
    def _():
        mlp_ref[...] += mlp
        back_ref[...] += back


def ffn_call(x, grad, weights):
    tokens, model = x.shape
    blocks, quarters, parts, units, unused = weights.shape
    whole = lambda i: (0, 0)
    wide = pl.BlockSpec((blocks, 1, parts, units, LANES), lambda i: (0, i, 0, 0, 0))
    return pl.pallas_call(
        ffn_kernel,
        grid=(quarters,),
        in_specs=[pl.BlockSpec((tokens, model), whole), pl.BlockSpec((tokens, model), whole), wide],
        out_specs=[pl.BlockSpec((tokens, model), whole), pl.BlockSpec((tokens, model), whole), wide],
        out_shape=[
            jax.ShapeDtypeStruct((tokens, model), F32),
            jax.ShapeDtypeStruct((tokens, model), F32),
            jax.ShapeDtypeStruct(weights.shape, BF),
        ],
        compiler_params=pltpu.CompilerParams(vmem_limit_bytes=VMEM_LIMIT),
        cost_estimate=pl.CostEstimate(
            flops=18 * tokens * model * units * quarters,
            bytes_accessed=36 << 20,
            transcendentals=0,
        ),
        name="ffn",
    )(x, grad, weights)


def pieces_along(values, ways):
    here = values
    below, above = [], []
    up, down = here, here
    for hop in range(1, ways):
        up = lax.ppermute(up, "mp", [(i, i + 1) for i in range(hop - 1, ways - 1)])
        down = lax.ppermute(down, "mp", [(i, i - 1) for i in range(1, ways - hop + 1)])
        below.append(up)
        above.append(down)
    line = jnp.concatenate(below[::-1] + [here] + above, axis=0)
    rows = values.shape[0]
    at = (ways - 1 - lax.axis_index("mp")) * rows
    return lax.dynamic_slice_in_dim(line, at, ways * rows, axis=0)


def swap_rows(values, ways):
    rows = values.shape[0] // ways
    me = lax.axis_index("mp")
    blocks = values.reshape(ways, rows, values.shape[1])
    out = jnp.zeros_like(blocks)
    own = lax.dynamic_index_in_dim(blocks, me, 0, keepdims=False)
    out = lax.dynamic_update_index_in_dim(out, own, me, 0)
    for k in range(1, ways):
        sent = lax.dynamic_index_in_dim(blocks, (me + k) % ways, 0, keepdims=False)
        got = lax.ppermute(sent, "mp", [(i, (i + k) % ways) for i in range(ways)])
        out = lax.dynamic_update_index_in_dim(out, got, (me - k) % ways, 0)
    return out


def add_low(a, b):
    return (a.astype(F32) + b.astype(F32)).astype(BF)


def pick(values, at, axis):
    return lax.dynamic_index_in_dim(values, at, axis, keepdims=False)


def sum_slabs(values):
    dp = lax.axis_index("dp")
    core, x, y = dp % 2, (dp // 2) % 2, dp // 4
    flip = lambda bit: [(i, i ^ bit) for i in range(8)]
    rows = values.shape[2]
    g = values.reshape(2, 2, 2, 4, rows, LANES)
    g = add_low(pick(g, core, 2), lax.ppermute(pick(g, 1 - core, 2), "dp", flip(1)))
    a, b = g[:, :, :2], g[:, :, 2:]
    a = add_low(pick(a, x, 1), lax.ppermute(pick(a, 1 - x, 1), "dp", flip(2)))
    b = add_low(pick(b, y, 0), lax.ppermute(pick(b, 1 - y, 0), "dp", flip(4)))
    a = add_low(pick(a, y, 0), lax.ppermute(pick(a, 1 - y, 0), "dp", flip(4)))
    b = add_low(pick(b, x, 0), lax.ppermute(pick(b, 1 - x, 0), "dp", flip(2)))
    g = jnp.concatenate([a, b], axis=0)
    me = lax.axis_index("mp")
    total = pick(g, me, 0).astype(F32)
    for k in range(1, 4):
        sent = pick(g, (me + k) % 4, 0)
        total += lax.ppermute(sent, "mp", [(i, (i + k) % 4) for i in range(4)]).astype(F32)
    return total


def sum_small(values, sizes):
    for axis, size in sizes:
        total = values
        for k in range(1, size):
            total += lax.ppermute(values, axis, [(i, (i + k) % size) for i in range(size)])
        values = total
    return values


def local(
    sizes,
    layer_input,
    segment_ids,
    grad_out,
    qkv_weight,
    attn_weight,
    inner_weight,
    outer_weight,
    attn_gain,
    mlp_gain,
):
    dps, mps = sizes
    rows, model = layer_input.shape
    segment = segment_ids[0]
    length = segment.shape[0]
    head_cols = qkv_weight.shape[2]
    units = inner_weight.shape[2]
    wide = model // LANES
    me = lax.axis_index("mp")
    my_start = me * rows
    tokens = layer_input.astype(F32)

    part = jnp.concatenate(
        [inner_weight.transpose(1, 2, 0), outer_weight.T[None]], axis=0
    )
    attn_part = attn_weight.T
    qkv_part = qkv_weight.reshape(qkv_weight.shape[0], 3 * head_cols)
    qkv_mine = lax.all_gather(qkv_part, "dp", axis=0, tiled=True)

    def every(values):
        got = lax.all_gather(values, ("dp", "mp"), axis=0)
        if dps != wide:
            lanes = values.shape[-1]
            got = got.reshape((dps, mps) + values.shape)
            got = got.reshape((wide, dps // wide, mps) + values.shape)
            got = jnp.moveaxis(got, 1, -2)
            return got.reshape((wide, mps) + values.shape[:-1] + (LANES,))
        return got.reshape((dps, mps) + values.shape)

    def shared(values):
        if dps == wide:
            return sum_slabs(values)
        lanes = LANES * wide // dps
        cut = values.reshape(values.shape[:-1] + (dps // wide, lanes))
        cut = jnp.moveaxis(cut, -2, 1).reshape((dps * mps,) + values.shape[2:-1] + (lanes,))
        return lax.psum_scatter(
            cut.astype(F32), ("dp", "mp"), scatter_dimension=0, tiled=True
        )[0]

    attn_all = every(attn_part)
    ffn_all = every(part)
    attn_t = attn_all.transpose(1, 2, 0, 3).reshape(model, model)

    cosine, sine = rope_tables(segment)
    lane = jnp.arange(LANES, dtype=jnp.int32) % HEAD_DIM
    same = segment[:, None] == lane[None, :]
    qaux = jnp.where(same | (lane >= 16)[None, :], 0.0, -BIG).astype(BF)
    kaux = jnp.where(same & (lane < 16)[None, :], 1.0, 0.0)
    kaux = jnp.where(((lane >= 16) & (lane < 19))[None, :], 1.0, kaux).astype(BF)
    live = (segment != 0).astype(F32)[:, None]
    live_mine = lax.dynamic_slice_in_dim(live, my_start, rows)

    x_all = pieces_along(layer_input, mps)
    normed_all, q, k, v = qkv_call(x_all, attn_gain[None], qkv_mine, cosine, sine)

    pairs = head_cols // LANES
    kept, heads = [], []
    for pair in range(pairs):
        o, qa, ka = attn_fwd_call(q, k, v, qaux, kaux, live, pair)
        kept.append((o, qa, ka))
        heads.append(swap_rows(o, mps))
    heads_out = jnp.stack(heads, axis=1)
    heads_out = heads_out.transpose(2, 0, 1, 3).reshape(rows, model)
    attn_out = dot_nn(heads_out, attn_t)
    middle = tokens + attn_out
    vhat, scale = norm_stats(middle)
    inner_in = (vhat * mlp_gain).astype(BF)
    mlp_out, inner_in_grad, ffn_grad = ffn_call(inner_in, grad_out, ffn_all)
    layer_output = (middle + mlp_out).astype(BF)
    squares = jnp.stack(
        [jnp.sum(live_mine * a * a) for a in (tokens, attn_out, middle, mlp_out)]
        + [jnp.sum(live_mine)]
    )
    ffn_sum = shared(ffn_grad.reshape(wide, mps, 3 * units, LANES)).reshape(3, units, -1)

    mlp_gain_part = jnp.sum(inner_in_grad * vhat, axis=0)
    middle_grad = grad_out.astype(F32) + norm_back(vhat, scale, mlp_gain, inner_in_grad)
    middle_low = middle_grad.astype(BF)
    heads_grad = dot_nt(middle_low, attn_t).astype(BF)
    attn_grad = dot_tn(heads_out, middle_low).astype(BF)
    attn_slab = attn_grad.reshape(mps, model // mps, wide, LANES).transpose(2, 0, 1, 3)
    attn_sum = shared(attn_slab)

    by_owner = heads_grad.reshape(rows, mps, pairs, LANES)
    returned, own = [], []
    for pair in range(pairs):
        sent = by_owner[:, :, pair].transpose(1, 0, 2).reshape(mps * rows, LANES)
        grad = swap_rows(sent, mps).reshape(length, LANES)
        o, qa, ka = kept[pair]
        parts = attn_bwd_call(qa, ka, v, grad, o, cosine, sine, pair)
        low = jnp.concatenate(parts, axis=1)
        own.append(parts)
        returned.append(swap_rows(low, mps))
    qkv_low = jnp.concatenate([own[p][c] for c in range(3) for p in range(pairs)], axis=1)
    qkv_grad = dot_tn(normed_all, qkv_low)
    qkv_sum = lax.psum_scatter(qkv_grad, "dp", scatter_dimension=0, tiled=True)

    qkv_full = lax.all_gather(qkv_part, ("dp", "mp"), axis=0).reshape(
        dps, mps, -1, 3, pairs, LANES
    )
    normed_grad = jnp.zeros((rows, model), F32)
    for pair in range(pairs):
        w = qkv_full[:, :, :, :, pair].transpose(1, 3, 4, 0, 2).reshape(mps, 3 * LANES, model)
        for z in range(mps):
            normed_grad += dot_nn(returned[pair][z], w[z])
    vhat_in, scale_in = norm_stats(tokens)
    attn_gain_part = jnp.sum(normed_grad * vhat_in, axis=0)
    input_grad = middle_grad + norm_back(vhat_in, scale_in, attn_gain, normed_grad)

    small = jnp.stack([attn_gain_part, mlp_gain_part, jnp.pad(squares, (0, model - 5))])
    if dps == wide:
        small = sum_small(small, (("dp", dps), ("mp", mps)))
    else:
        small = lax.psum(small, ("dp", "mp"))
    rms_values = jnp.sqrt(small[2, :4] / (small[2, 4] * model))
    return (
        layer_output,
        input_grad,
        qkv_sum.reshape(-1, 3, head_cols),
        attn_sum.T,
        ffn_sum[:2].transpose(2, 0, 1),
        ffn_sum[2].T,
        small[0],
        small[1],
        rms_values,
    )


def solution(mesh):
    sizes = (mesh.shape["dp"], mesh.shape["mp"])
    return jax.shard_map(
        functools.partial(local, sizes),
        mesh=mesh,
        in_specs=(
            P(("dp", "mp"), None),
            P("dp", None),
            P(("dp", "mp"), None),
            P("dp", None, "mp"),
            P("dp", "mp"),
            P("dp", None, "mp"),
            P("dp", "mp"),
            P(),
            P(),
        ),
        out_specs=(
            P(("dp", "mp"), None),
            P(("dp", "mp"), None),
            P("dp", None, "mp"),
            P("dp", "mp"),
            P("dp", None, "mp"),
            P("dp", "mp"),
            P(),
            P(),
            P(),
        ),
        check_vma=False,
    )
```

time: 1500 us -> 708 us (0.47)
  waiting for transfers between devices: 930 us -> 263 us
  matrix products: 279 us -> 30.5 us
  Pallas kernels: 0 us -> 142 us
  other arithmetic: 127 us -> 38.5 us
  starting transfers between devices: 1.48 us -> 74.4 us
  local copies, waits for them, and re-layouts: 71.7 us -> 133 us
  blocking collectives: 54 us -> 0 us
    reduce_scatter x8 -> x1, waiting for transfers between devices: 542 us -> 0.01 us  [local(): qkv_sum = lax.psum_scatter(qkv_grad, 'dp', scatter_dimension=0, tiled=True)]
    all_gather x7 -> x4, waiting for transfers between devices: 387 us -> 48.6 us  [the longest x2 48.6 us: every(): got = lax.all_gather(values, ('dp', 'mp'), axis=0)]
    dot_general x40 -> x12, matrix products: 279 us -> 30.5 us  [the longest x9 18.3 us: dot_nn(): lax.dot_general(a, b, (((1,), (0,)), ((), ())), preferred_element_type=F32)]
    ppermute x0 -> x50, waiting for transfers between devices: none -> 214 us  [the longest x3 50.9 us: pieces_along(): lax.ppermute(down, 'mp', [(i, i - 1) for i in range(1, ways - hop + 1)])]
    pallas_call x0 -> x6, Pallas kernels: none -> 142 us  [the longest x2 58.2 us: attn_bwd_call(): pl.pallas_call(attn_bwd_kernel, grid=(tokens // rows,), in_specs=[pl.Bloc...]
    ppermute x0 -> x50, starting transfers between devices: none -> 74.2 us  [the longest x18 27.5 us: swap_rows(): got = lax.ppermute(sent, 'mp', [(i, (i + k) % ways) for i in range(ways)])]
    slice x3 -> x20, local copies, waits for them, and re-layouts: 0.71 us -> 50.4 us  [the longest x10 26.6 us: local(): normed_grad += dot_nn(returned[pair][z], w[z])]
    psum x1 -> x0, blocking collectives: 41 us -> none  [local(): lax.psum((squares, live_count, attn_gain_part, mlp_gain_part), ('dp', 'mp'))]
  transfers between devices with their start and end apart: 15 -> 55, of which waited for: 14 -> 16; matrix products, arithmetic and copies ran while one was open for 5% -> 25% of each run, Pallas kernels for 0% -> 15%
where the time goes in v1:
time: 708 us; the launch traced here: 697 us
  waiting for transfers between devices  263 us (37%)
  Pallas kernels  142 us (20%)
  local copies, waits for them, and re-layouts  133 us (19%)
  starting transfers between devices  74.4 us (11%)
  other arithmetic  38.5 us (5%)
  matrix products  30.5 us (4%)
  between operations  15.9 us (2%)
    pallas_call x2, Pallas kernels, attn_bwd_call(): pl.pallas_call(attn_bwd_kernel, grid=(tokens // rows,), in_specs=[pl.Bloc...  58.2 us
    ppermute x3, waiting for transfers between devices, pieces_along(): lax.ppermute(down, 'mp', [(i, i - 1) for i in range(1, ways - hop + 1)])  50.9 us
    all_gather x2, waiting for transfers between devices, every(): got = lax.all_gather(values, ('dp', 'mp'), axis=0)  48.6 us
    ppermute x6, waiting for transfers between devices, sum_slabs(): lax.ppermute(sent, 'mp', [(i, (i + k) % 4) for i in range(4)]).astype(F32)  41 us
    pallas_call x2, Pallas kernels, attn_fwd_call(): pl.pallas_call(attn_fwd_kernel, grid=(tokens // rows,), in_specs=[pl.Bloc...  38 us
    pallas_call x1, Pallas kernels, ffn_call(): pl.pallas_call(ffn_kernel, grid=(quarters,), in_specs=[pl.BlockSpec((toke...  35.9 us
    ppermute x2, waiting for transfers between devices, sum_slabs(): b = add_low(pick(b, y, 0), lax.ppermute(pick(b, 1 - y, 0), 'dp', flip(4)))  32.4 us
    ppermute x18, waiting for transfers between devices, swap_rows(): got = lax.ppermute(sent, 'mp', [(i, (i + k) % ways) for i in range(ways)])  31.6 us
  transfers between devices with their start and end apart: 55, of which 16 were waited for; matrix products, arithmetic and copies ran while one was open for 25% of the time, Pallas kernels for 15%

profile of v1, /device:TPU:0, one launch (start us, length us, event | category | flops | bytes accessed | tf_op | source)
XLA Modules:
  0.0 697.1 jit_solution(17285811661815247063)
XLA Ops:
  12.9 5.0 collective-permute-start
  19.9 20.4 %collective-permute-done = bf16[512,1024]{1,0:T(8,128)(2,1)S(1)} collective-permute-done((bf16[512,1024]{1,0:T(8,128)(2,1)S(1)}, bf16[512,1024]{1,0:T(8,128)(2,1)S(1)}, u32[]{:S(2)}, u32[]{:S(2)}) %collective-permute-start) | collective-permute-done | bytes 1048608 | tf_op jit(solution)/shard_map/ppermute | solution.py:377
  48.8 5.5 negate_select_fusion
  54.4 20.7 %collective-permute-done.4 = bf16[512,1024]{1,0:T(8,128)(2,1)} collective-permute-done((bf16[512,1024]{1,0:T(8,128)(2,1)S(1)}, bf16[512,1024]{1,0:T(8,128)(2,1)}, u32[]{:S(2)}, u32[]{:S(2)}) %collective-permute-start.4) | collective-permute-done | bytes 1048608 | tf_op jit(solution)/shard_map/ppermute | solution.py:378
  79.3 29.1 %collective-permute-done.5 = bf16[512,1024]{1,0:T(8,128)(2,1)S(1)} collective-permute-done((bf16[512,1024]{1,0:T(8,128)(2,1)}, bf16[512,1024]{1,0:T(8,128)(2,1)S(1)}, u32[]{:S(2)}, u32[]{:S(2)}) %collective-permute-start.5) | collective-permute-done | bytes 1048608 | tf_op jit(solution)/shard_map/ppermute | solution.py:378
  110.9 9.6 %qkv.1 = (bf16[2048,1024]{1,0:T(8,128)(2,1)}, bf16[2048,256]{1,0:T(8,128)(2,1)}, bf16[2048,256]{1,0:T(8,128)(2,1)}, bf16[2048,256]{1,0:T(8,128)(2,1)}) custom-call(bf16[2048,1024]{1,0:T(8,128)(2,1)} %constant_dynamic-slice_fusion.16.x_ref, f32[1,1024]{1,0:T(1,128)} %bitcast.369, bf16[1024,768]{1,0:T(8,128)(2,1)} %all-gather.7.cloned.1.call-done.w_ref, ...), custom_call_target="tpu_custom_call" | custom-call | flops 3221225472 | bytes 16777216 | tf_op jit(solution)/shard_map/qkv/pallas_call | solution.py:97
  120.5 19.0 %attn_fwd.2 = (bf16[2048,128]{1,0:T(8,128)(2,1)}, bf16[2,2048,128]{2,1,0:T(8,128)(2,1)}, bf16[2,2048,128]{2,1,0:T(8,128)(2,1)}) custom-call(bf16[2048,256]{1,0:T(8,128)(2,1)} %get-tuple-element.28.q_ref, bf16[2048,256]{1,0:T(8,128)(2,1)} %get-tuple-element.29.k_ref, bf16[2048,256]{1,0:T(8,128)(2,1)} %get-tuple-element.30.v_ref, ...), custom_call_target="tpu_custom_call" | custom-call | flops 4294967296 | bytes 4194304 | tf_op jit(solution)/shard_map/attn_fwd/pallas_call | solution.py:178
  145.1 19.0 %attn_fwd.3 = (bf16[2048,128]{1,0:T(8,128)(2,1)}, bf16[2,2048,128]{2,1,0:T(8,128)(2,1)}, bf16[2,2048,128]{2,1,0:T(8,128)(2,1)}) custom-call(bf16[2048,256]{1,0:T(8,128)(2,1)} %get-tuple-element.28.q_ref, bf16[2048,256]{1,0:T(8,128)(2,1)} %get-tuple-element.29.k_ref, bf16[2048,256]{1,0:T(8,128)(2,1)} %get-tuple-element.30.v_ref, ...), custom_call_target="tpu_custom_call" | custom-call | flops 4294967296 | bytes 4194304 | tf_op jit(solution)/shard_map/attn_fwd/pallas_call | solution.py:178
  171.3 4.7 collective-permute-done.9
  176.0 6.9 collective-permute-done.10
  187.5 4.3 copy.96
  191.8 4.8 fusion.93
  198.6 8.7 %copy.100 = bf16[32,128,768]{1,2,0:T(8,128)(2,1)} copy(bf16[32,128,768]{2,1,0:T(8,128)(2,1)} %all-gather.9.cloned.1.call-done) | data formatting | bytes 12582912 | tf_op jit(solution)/shard_map/all_gather | solution.py:547
  207.2 8.2 %fusion.95 = (bf16[8,4,128,3,1,128]{2,5,4,3,1,0:T(8,128)(2,1)}, bf16[8,4,128,3,1,128]{2,5,4,3,1,0:T(8,128)(2,1)}) fusion(bf16[8,4,128,3,2,128]{2,5,4,3,1,0:T(8,128)(2,1)} %bitcast.318), kind=kLoop, calls=%fused_computation.259 | loop fusion | bytes 12582912 | tf_op jit(solution)/shard_map/slice | solution.py:552
  215.4 4.7 copy.101
  233.3 4.7 copy.107
  251.3 48.6 %all-gather.13.cloned.1.call-done = bf16[96,656,128]{2,1,0:T(8,128)(2,1)} async-done(((bf16[3,656,128]{2,1,0:T(8,128)(2,1)}), bf16[96,656,128]{2,1,0:T(8,128)(2,1)}) %all-gather.13.cloned.1.call-update) | async-done | bytes 16121872 | tf_op jit(solution)/shard_map/all_gather | solution.py:470
  300.0 35.9 %ffn.1 = (f32[512,1024]{1,0:T(8,128)}, f32[512,1024]{1,0:T(8,128)}, bf16[8,4,3,656,128]{4,3,2,1,0:T(8,128)(2,1)}) custom-call(bf16[512,1024]{1,0:T(8,128)(2,1)} %multiply_convert_fusion.x_ref, bf16[512,1024]{1,0:T(8,128)(2,1)} %g_ref.1, bf16[8,4,3,656,128]{4,3,2,1,0:T(8,128)(2,1)} %bitcast.372), custom_call_target="tpu_custom_call" | custom-call | flops 24763170816 | bytes 37748736 | tf_op jit(solution)/shard_map/ffn/pallas_call | solution.py:352
  365.3 7.1 %dynamic-slice_bitcast_fusion = bf16[2,2,4,1968,128]{4,3,2,1,0:T(8,128)(2,1)} fusion(bf16[2,2,2,4,1968,128]{5,4,3,2,1,0:T(8,128)(2,1)} %bitcast.319, s32[]{:T(128)S(6)} %select_n.325), kind=kLoop, calls=%fused_computation.2 | loop fusion | bytes 16121860 | tf_op jit(solution)/shard_map/jit(dynamic_index_in_dim)/squeeze | solution.py:406
  381.7 29.0 %attn_bwd.2 = (bf16[2048,128]{1,0:T(8,128)(2,1)}, bf16[2048,128]{1,0:T(8,128)(2,1)}, bf16[2048,128]{1,0:T(8,128)(2,1)}) custom-call(bf16[2,2048,128]{2,1,0:T(8,128)(2,1)} %get-tuple-element.35.qa_ref, bf16[2,2048,128]{2,1,0:T(8,128)(2,1)} %get-tuple-element.36.ka_ref, bf16[2048,256]{1,0:T(8,128)(2,1)} %get-tuple-element.30.v_ref, ...), custom_call_target="tpu_custom_call" | custom-call | flops 10737418240 | bytes 6291456 | tf_op jit(solution)/shard_map/attn_bwd/pallas_call | solution.py:271
  423.9 29.2 %attn_bwd.3 = (bf16[2048,128]{1,0:T(8,128)(2,1)}, bf16[2048,128]{1,0:T(8,128)(2,1)}, bf16[2048,128]{1,0:T(8,128)(2,1)}) custom-call(bf16[2,2048,128]{2,1,0:T(8,128)(2,1)} %get-tuple-element.40.qa_ref, bf16[2,2048,128]{2,1,0:T(8,128)(2,1)} %get-tuple-element.41.ka_ref, bf16[2048,256]{1,0:T(8,128)(2,1)} %get-tuple-element.30.v_ref, ...), custom_call_target="tpu_custom_call" | custom-call | flops 10737418240 | bytes 6291456 | tf_op jit(solution)/shard_map/attn_bwd/pallas_call | solution.py:271
  461.2 7.4 %fusion.101 = f32[1024,768]{1,0:T(8,128)} fusion(bf16[2048,1024]{1,0:T(8,128)(2,1)} %get-tuple-element.45, bf16[2048,768]{1,0:T(8,128)(2,1)S(1)} %copy-done.29), kind=kOutput, calls=%fused_computation.265 | convolution fusion | flops 3221225472 | bytes 10485760 | tf_op jit(solution)/shard_map/dot_general | solution.py:30
  479.3 5.0 collective-permute-done.21
  484.3 14.9 %collective-permute-done.22 = bf16[512,384]{1,0:T(8,128)(2,1)S(1)} collective-permute-done((bf16[512,384]{1,0:T(8,128)(2,1)S(1)}, bf16[512,384]{1,0:T(8,128)(2,1)S(1)}, u32[]{:S(2)}, u32[]{:S(2)}) %collective-permute-start.22) | collective-permute-done | bytes 393248 | tf_op jit(solution)/shard_map/ppermute | solution.py:396
  510.5 4.2 fusion.12
  521.0 4.2 fusion.11
  526.6 6.8 fusion
  539.5 8.7 %collective-permute-start.47 = (f32[3,1024]{1,0:T(4,128)S(1)}, f32[3,1024]{1,0:T(4,128)S(1)}, u32[]{:S(2)}, u32[]{:S(2)}) collective-permute-start(f32[3,1024]{1,0:T(4,128)S(1)} %add_add_fusion.2), channel_id=1, source_target_pairs={{0,1},{1,2},{2,3},{3,0},{4,5},{5,6},{6,7},{7,4},{8,9},{9,10},{10,1... | collective-permute-start | bytes 36872 | tf_op jit(solution)/shard_map/ppermute | solution.py:434
  555.5 32.4 %collective-permute-done.27 = bf16[2,2,256,128]{3,2,1,0:T(8,128)(2,1)S(1)} collective-permute-done((bf16[2,2,256,128]{3,2,1,0:T(8,128)(2,1)S(1)}, bf16[2,2,256,128]{3,2,1,0:T(8,128)(2,1)S(1)}, u32[]{:S(2)}, u32[]{:S(2)}) %collective-permute-start.27) | collective-permute-done | bytes 262176 | tf_op jit(solution)/shard_map/ppermute | solution.py:418
  589.5 15.2 %collective-permute-done.25 = bf16[2,2,256,128]{3,2,1,0:T(8,128)(2,1)S(1)} collective-permute-done((bf16[2,2,256,128]{3,2,1,0:T(8,128)(2,1)S(1)}, bf16[2,2,256,128]{3,2,1,0:T(8,128)(2,1)S(1)}, u32[]{:S(2)}, u32[]{:S(2)}) %collective-permute-start.25) | collective-permute-done | bytes 262176 | tf_op jit(solution)/shard_map/ppermute | solution.py:417
  610.4 19.5 %collective-permute-done.36 = bf16[2,1968,128]{2,1,0:T(8,128)(2,1)S(1)} collective-permute-done((bf16[2,1968,128]{2,1,0:T(8,128)(2,1)S(1)}, bf16[2,1968,128]{2,1,0:T(8,128)(2,1)S(1)}, u32[]{:S(2)}, u32[]{:S(2)}) %collective-permute-start.36) | collective-permute-done | bytes 1007648 | tf_op jit(solution)/shard_map/ppermute | solution.py:420
  642.9 41.0 %collective-permute-done.30 = bf16[256,128]{1,0:T(8,128)(2,1)S(1)} collective-permute-done((bf16[256,128]{1,0:T(8,128)(2,1)S(1)}, bf16[256,128]{1,0:T(8,128)(2,1)S(1)}, u32[]{:S(2)}, u32[]{:S(2)}) %collective-permute-start.30) | collective-permute-done | bytes 65568 | tf_op jit(solution)/shard_map/ppermute | solution.py:426
  (322 shorter events, 196.9 us)
Async XLA Ops:
  7.2 103.7 %all-gather.7.cloned.1.call-start = ((), (), s32[]{:S(2)}) async-start(), calls=%async_computation.1 | async-start | bytes 1769472 | tf_op jit(solution)/shard_map/all_gather | solution.py:467
  9.3 174.9 %all-gather.11.cloned.1.call-start = ((), (), s32[]{:S(2)}) async-start(), calls=%async_computation.4 | async-start | bytes 2162688 | tf_op jit(solution)/shard_map/all_gather | solution.py:470
  10.0 188.5 %all-gather.9.cloned.1.call-start = ((), (), s32[]{:S(2)}) async-start(), calls=%async_computation.2 | async-start | bytes 6488064 | tf_op jit(solution)/shard_map/all_gather | solution.py:547
  10.9 289.0 %all-gather.13.cloned.1.call-start = ((), (), s32[]{:S(2)}) async-start(), calls=%async_computation.5 | async-start | bytes 16625664 | tf_op jit(solution)/shard_map/all_gather | solution.py:470
  12.9 671.9 %reduce-scatter.2.cloned.1.call-start = ((), (), s32[]{:S(2)}) async-start(), calls=%async_computation.3 | async-start | bytes 3538944 | tf_op jit(solution)/shard_map/reduce_scatter | solution.py:545
  12.9 27.3 %collective-permute-start = (bf16[512,1024]{1,0:T(8,128)(2,1)S(1)}, bf16[512,1024]{1,0:T(8,128)(2,1)S(1)}, u32[]{:S(2)}, u32[]{:S(2)}) collective-permute-start(bf16[512,1024]{1,0:T(8,128)(2,1)S(1)} %copy-done), channel_id=1, source_target_pairs={{0,1},{1,2},{2,3},{4,5},{5,6},{6,7},{8,9},{9,10},{10,11},{12,13},{... | collective-permute-start | bytes 3145736 | tf_op jit(solution)/shard_map/ppermute | solution.py:377
  17.9 26.5 %collective-permute-start.3 = (bf16[512,1024]{1,0:T(8,128)(2,1)S(1)}, bf16[512,1024]{1,0:T(8,128)(2,1)S(1)}, u32[]{:S(2)}, u32[]{:S(2)}) collective-permute-start(bf16[512,1024]{1,0:T(8,128)(2,1)S(1)} %copy-done), channel_id=1, source_target_pairs={{1,0},{2,1},{3,2},{5,4},{6,5},{7,6},{9,8},{10,9},{11,10},{13,12},{... | collective-permute-start | bytes 3145736 | tf_op jit(solution)/shard_map/ppermute | solution.py:378
  44.5 30.6 %collective-permute-start.4 = (bf16[512,1024]{1,0:T(8,128)(2,1)S(1)}, bf16[512,1024]{1,0:T(8,128)(2,1)}, u32[]{:S(2)}, u32[]{:S(2)}) collective-permute-start(bf16[512,1024]{1,0:T(8,128)(2,1)S(1)} %collective-permute-done.3), channel_id=1, source_target_pairs={{1,0},{2,1},{5,4},{6,5},{9,8},{10,9},{13,12},{14,13},{17,16},{18,1... | collective-permute-start | bytes 3145736 | tf_op jit(solution)/shard_map/ppermute | solution.py:378
  48.0 28.4 %collective-permute-start.2 = (bf16[512,1024]{1,0:T(8,128)(2,1)}, bf16[512,1024]{1,0:T(8,128)(2,1)S(1)}, u32[]{:S(2)}, u32[]{:S(2)}) collective-permute-start(bf16[512,1024]{1,0:T(8,128)(2,1)} %collective-permute-done.1), channel_id=1, source_target_pairs={{2,3},{6,7},{10,11},{14,15},{18,19},{22,23},{26,27},{30,31}} | collective-permute-start | bytes 3145736 | tf_op jit(solution)/shard_map/ppermute | solution.py:377
  75.1 33.3 %collective-permute-start.5 = (bf16[512,1024]{1,0:T(8,128)(2,1)}, bf16[512,1024]{1,0:T(8,128)(2,1)S(1)}, u32[]{:S(2)}, u32[]{:S(2)}) collective-permute-start(bf16[512,1024]{1,0:T(8,128)(2,1)} %collective-permute-done.4), channel_id=1, source_target_pairs={{1,0},{5,4},{9,8},{13,12},{17,16},{21,20},{25,24},{29,28}} | collective-permute-start | bytes 3145736 | tf_op jit(solution)/shard_map/ppermute | solution.py:378
  140.9 27.2 %collective-permute-start.6 = (bf16[512,128]{0,1:T(8,128)(2,1)S(1)}, bf16[512,128]{0,1:T(8,128)(2,1)S(1)}, u32[]{:S(2)}, u32[]{:S(2)}) collective-permute-start(bf16[512,128]{0,1:T(8,128)(2,1)S(1)} %bitcast.358), channel_id=1, source_target_pairs={{0,1},{1,2},{2,3},{3,0},{4,5},{5,6},{6,7},{7,4},{8,9},{9,10},{10,1... | collective-permute-start | bytes 393224 | tf_op jit(solution)/shard_map/ppermute | solution.py:396
  141.1 34.9 %collective-permute-start.7 = (bf16[512,128]{0,1:T(8,128)(2,1)S(1)}, bf16[512,128]{0,1:T(8,128)(2,1)S(1)}, u32[]{:S(2)}, u32[]{:S(2)}) collective-permute-start(bf16[512,128]{0,1:T(8,128)(2,1)S(1)} %bitcast.357), channel_id=1, source_target_pairs={{0,2},{1,3},{2,0},{3,1},{4,6},{5,7},{6,4},{7,5},{8,10},{9,11},{10,... | collective-permute-start | bytes 393224 | tf_op jit(solution)/shard_map/ppermute | solution.py:396
  143.3 39.7 %collective-permute-start.8 = (bf16[512,128]{0,1:T(8,128)(2,1)S(1)}, bf16[512,128]{0,1:T(8,128)(2,1)S(1)}, u32[]{:S(2)}, u32[]{:S(2)}) collective-permute-start(bf16[512,128]{0,1:T(8,128)(2,1)S(1)} %bitcast.356), channel_id=1, source_target_pairs={{0,3},{1,0},{2,1},{3,2},{4,7},{5,4},{6,5},{7,6},{8,11},{9,8},{10,9... | collective-permute-start | bytes 393224 | tf_op jit(solution)/shard_map/ppermute | solution.py:396
  359.6 57.1 %collective-permute-start.18 = (bf16[512,128]{1,0:T(8,128)(2,1)S(1)}, bf16[512,128]{1,0:T(8,128)(2,1)}, u32[]{:S(2)}, u32[]{:S(2)}) collective-permute-start(bf16[512,128]{1,0:T(8,128)(2,1)S(1)} %bitcast.353), channel_id=1, source_target_pairs={{0,1},{1,2},{2,3},{3,0},{4,5},{5,6},{6,7},{7,4},{8,9},{9,10},{10,1... | collective-permute-start | bytes 393224 | tf_op jit(solution)/shard_map/ppermute | solution.py:396
  360.3 57.3 %collective-permute-start.19 = (bf16[512,128]{1,0:T(8,128)(2,1)}, bf16[512,128]{1,0:T(8,128)(2,1)}, u32[]{:S(2)}, u32[]{:S(2)}) collective-permute-start(bf16[512,128]{1,0:T(8,128)(2,1)} %bitcast.312), channel_id=1, source_target_pairs={{0,2},{1,3},{2,0},{3,1},{4,6},{5,7},{6,4},{7,5},{8,10},{9,11},{10,... | collective-permute-start | bytes 393224 | tf_op jit(solution)/shard_map/ppermute | solution.py:396
  373.6 46.6 %collective-permute-start.20 = (bf16[512,128]{1,0:T(8,128)(2,1)}, bf16[512,128]{1,0:T(8,128)(2,1)S(1)}, u32[]{:S(2)}, u32[]{:S(2)}) collective-permute-start(bf16[512,128]{1,0:T(8,128)(2,1)} %bitcast.311), channel_id=1, source_target_pairs={{0,3},{1,0},{2,1},{3,2},{4,7},{5,4},{6,5},{7,6},{8,11},{9,8},{10,9... | collective-permute-start | bytes 393224 | tf_op jit(solution)/shard_map/ppermute | solution.py:396
  378.0 147.2 %collective-permute-start.32 = (bf16[2,2,4,1968,128]{4,3,2,1,0:T(8,128)(2,1)}, bf16[2,2,4,1968,128]{4,3,2,1,0:T(8,128)(2,1)}, u32[]{:S(2)}, u32[]{:S(2)}) collective-permute-start(bf16[2,2,4,1968,128]{4,3,2,1,0:T(8,128)(2,1)} %dynamic-slice_bitcast_fusion), channel_id=1, source_target_pairs={{0,4},{4,0},{8,12},{12,8},{16,20},{20,16},{24,28},{28,24},{1,5},{5... | collective-permute-start | bytes 24182792 | tf_op jit(solution)/shard_map/ppermute | solution.py:415
  379.6 171.0 %collective-permute-start.24 = (bf16[2,2,4,256,128]{4,3,2,1,0:T(8,128)(2,1)}, bf16[2,2,4,256,128]{4,3,2,1,0:T(8,128)(2,1)}, u32[]{:S(2)}, u32[]{:S(2)}) collective-permute-start(bf16[2,2,4,256,128]{4,3,2,1,0:T(8,128)(2,1)} %dynamic-slice_bitcast_fusion.3), channel_id=1, source_target_pairs={{0,4},{4,0},{8,12},{12,8},{16,20},{20,16},{24,28},{28,24},{1,5},{5... | collective-permute-start | bytes 3145736 | tf_op jit(solution)/shard_map/ppermute | solution.py:415
  416.7 53.6 %collective-permute-start.15 = (bf16[512,384]{1,0:T(8,128)(2,1)}, bf16[512,384]{1,0:T(8,128)(2,1)S(1)}, u32[]{:S(2)}, u32[]{:S(2)}) collective-permute-start(bf16[512,384]{1,0:T(8,128)(2,1)} %get-tuple-element.115), channel_id=1, source_target_pairs={{0,1},{1,2},{2,3},{3,0},{4,5},{5,6},{6,7},{7,4},{8,9},{9,10},{10,1... | collective-permute-start | bytes 1179656 | tf_op jit(solution)/shard_map/ppermute | solution.py:396
  417.7 53.5 %collective-permute-start.16 = (bf16[512,384]{1,0:T(8,128)(2,1)}, bf16[512,384]{1,0:T(8,128)(2,1)}, u32[]{:S(2)}, u32[]{:S(2)}) collective-permute-start(bf16[512,384]{1,0:T(8,128)(2,1)} %get-tuple-element.114), channel_id=1, source_target_pairs={{0,2},{1,3},{2,0},{3,1},{4,6},{5,7},{6,4},{7,5},{8,10},{9,11},{10,... | collective-permute-start | bytes 1179656 | tf_op jit(solution)/shard_map/ppermute | solution.py:396
  420.1 54.2 %collective-permute-start.17 = (bf16[512,384]{1,0:T(8,128)(2,1)}, bf16[512,384]{1,0:T(8,128)(2,1)}, u32[]{:S(2)}, u32[]{:S(2)}) collective-permute-start(bf16[512,384]{1,0:T(8,128)(2,1)} %get-tuple-element.113), channel_id=1, source_target_pairs={{0,3},{1,0},{2,1},{3,2},{4,7},{5,4},{6,5},{7,6},{8,11},{9,8},{10,9... | collective-permute-start | bytes 1179656 | tf_op jit(solution)/shard_map/ppermute | solution.py:396
  471.1 28.1 %collective-permute-start.22 = (bf16[512,384]{1,0:T(8,128)(2,1)S(1)}, bf16[512,384]{1,0:T(8,128)(2,1)S(1)}, u32[]{:S(2)}, u32[]{:S(2)}) collective-permute-start(bf16[512,384]{1,0:T(8,128)(2,1)S(1)} %get-tuple-element.118), channel_id=1, source_target_pairs={{0,2},{1,3},{2,0},{3,1},{4,6},{5,7},{6,4},{7,5},{8,10},{9,11},{10,... | collective-permute-start | bytes 1179656 | tf_op jit(solution)/shard_map/ppermute | solution.py:396
  538.2 67.5 %collective-permute-start.35 = (bf16[2,2,1968,128]{3,2,1,0:T(8,128)(2,1)S(1)}, bf16[2,2,1968,128]{3,2,1,0:T(8,128)(2,1)S(1)}, u32[]{:S(2)}, u32[]{:S(2)}) collective-permute-start(bf16[2,2,1968,128]{3,2,1,0:T(8,128)(2,1)S(1)} %dynamic-slice_bitcast_fusion.1), channel_id=1, source_target_pairs={{0,16},{4,20},{8,24},{12,28},{16,0},{20,4},{24,8},{28,12},{1,17},{... | collective-permute-start | bytes 6045704 | tf_op jit(solution)/shard_map/ppermute | solution.py:418
  552.3 54.2 %collective-permute-start.33 = (bf16[2,2,1968,128]{3,2,1,0:T(8,128)(2,1)S(1)}, bf16[2,2,1968,128]{3,2,1,0:T(8,128)(2,1)S(1)}, u32[]{:S(2)}, u32[]{:S(2)}) collective-permute-start(bf16[2,2,1968,128]{3,2,1,0:T(8,128)(2,1)S(1)} %dynamic-slice_bitcast_fusion.2), channel_id=1, source_target_pairs={{0,8},{4,12},{8,0},{12,4},{16,24},{20,28},{24,16},{28,20},{1,9},{5... | collective-permute-start | bytes 6045704 | tf_op jit(solution)/shard_map/ppermute | solution.py:417
  553.4 34.5 %collective-permute-start.27 = (bf16[2,2,256,128]{3,2,1,0:T(8,128)(2,1)S(1)}, bf16[2,2,256,128]{3,2,1,0:T(8,128)(2,1)S(1)}, u32[]{:S(2)}, u32[]{:S(2)}) collective-permute-start(bf16[2,2,256,128]{3,2,1,0:T(8,128)(2,1)S(1)} %dynamic-slice_bitcast_fusion.12), channel_id=1, source_target_pairs={{0,16},{4,20},{8,24},{12,28},{16,0},{20,4},{24,8},{28,12},{1,17},{... | collective-permute-start | bytes 786440 | tf_op jit(solution)/shard_map/ppermute | solution.py:418
  554.1 50.7 %collective-permute-start.25 = (bf16[2,2,256,128]{3,2,1,0:T(8,128)(2,1)S(1)}, bf16[2,2,256,128]{3,2,1,0:T(8,128)(2,1)S(1)}, u32[]{:S(2)}, u32[]{:S(2)}) collective-permute-start(bf16[2,2,256,128]{3,2,1,0:T(8,128)(2,1)S(1)} %dynamic-slice_bitcast_fusion.13), channel_id=1, source_target_pairs={{0,8},{4,12},{8,0},{12,4},{16,24},{20,28},{24,16},{28,20},{1,9},{5... | collective-permute-start | bytes 786440 | tf_op jit(solution)/shard_map/ppermute | solution.py:417
  610.0 31.5 %collective-permute-start.29 = (bf16[256,128]{1,0:T(8,128)(2,1)S(1)}, bf16[256,128]{1,0:T(8,128)(2,1)S(1)}, u32[]{:S(2)}, u32[]{:S(2)}) collective-permute-start(bf16[256,128]{1,0:T(8,128)(2,1)S(1)} %get-tuple-element.142), channel_id=1, source_target_pairs={{0,1},{1,2},{2,3},{3,0},{4,5},{5,6},{6,7},{7,4},{8,9},{9,10},{10,1... | collective-permute-start | bytes 196616 | tf_op jit(solution)/shard_map/ppermute | solution.py:426
  633.8 53.1 %collective-permute-start.37 = (bf16[1968,128]{1,0:T(8,128)(2,1)}, bf16[1968,128]{1,0:T(8,128)(2,1)}, u32[]{:S(2)}, u32[]{:S(2)}) collective-permute-start(bf16[1968,128]{1,0:T(8,128)(2,1)} %get-tuple-element.110), channel_id=1, source_target_pairs={{0,1},{1,2},{2,3},{3,0},{4,5},{5,6},{6,7},{7,4},{8,9},{9,10},{10,1... | collective-permute-start | bytes 1511432 | tf_op jit(solution)/shard_map/ppermute | solution.py:426
  633.8 53.1 %collective-permute-start.38 = (bf16[1968,128]{1,0:T(8,128)(2,1)S(1)}, bf16[1968,128]{1,0:T(8,128)(2,1)}, u32[]{:S(2)}, u32[]{:S(2)}) collective-permute-start(bf16[1968,128]{1,0:T(8,128)(2,1)S(1)} %get-tuple-element.111), channel_id=1, source_target_pairs={{0,2},{1,3},{2,0},{3,1},{4,6},{5,7},{6,4},{7,5},{8,10},{9,11},{10,... | collective-permute-start | bytes 1511432 | tf_op jit(solution)/shard_map/ppermute | solution.py:426
  635.9 50.9 %collective-permute-start.39 = (bf16[1968,128]{1,0:T(8,128)(2,1)S(1)}, bf16[1968,128]{1,0:T(8,128)(2,1)}, u32[]{:S(2)}, u32[]{:S(2)}) collective-permute-start(bf16[1968,128]{1,0:T(8,128)(2,1)S(1)} %get-tuple-element.112), channel_id=1, source_target_pairs={{0,3},{1,0},{2,1},{3,2},{4,7},{5,4},{6,5},{7,6},{8,11},{9,8},{10,9... | collective-permute-start | bytes 1511432 | tf_op jit(solution)/shard_map/ppermute | solution.py:426
  639.4 44.5 %collective-permute-start.30 = (bf16[256,128]{1,0:T(8,128)(2,1)S(1)}, bf16[256,128]{1,0:T(8,128)(2,1)S(1)}, u32[]{:S(2)}, u32[]{:S(2)}) collective-permute-start(bf16[256,128]{1,0:T(8,128)(2,1)S(1)} %get-tuple-element.143), channel_id=1, source_target_pairs={{0,2},{1,3},{2,0},{3,1},{4,6},{5,7},{6,4},{7,5},{8,10},{9,11},{10,... | collective-permute-start | bytes 196616 | tf_op jit(solution)/shard_map/ppermute | solution.py:426
  641.5 42.4 %collective-permute-start.31 = (bf16[256,128]{1,0:T(8,128)(2,1)S(1)}, bf16[256,128]{1,0:T(8,128)(2,1)S(1)}, u32[]{:S(2)}, u32[]{:S(2)}) collective-permute-start(bf16[256,128]{1,0:T(8,128)(2,1)S(1)} %get-tuple-element.144), channel_id=1, source_target_pairs={{0,3},{1,0},{2,1},{3,2},{4,7},{5,4},{6,5},{7,6},{8,11},{9,8},{10,9... | collective-permute-start | bytes 196616 | tf_op jit(solution)/shard_map/ppermute | solution.py:426
  (55 other events, 501.6 us)
Sparse Core Ops, SparseCore 0:
  10.5 28.3 all-gather.6
  41.8 61.0 all-gather.10
  106.3 79.8 all-gather.8
  188.9 111.0 all-gather.12
  468.8 44.3 reduce-scatter.1

commit v2 on v1

v2 whole, which is shorter than its diff:
```python
import functools
import math

import jax
import jax.numpy as jnp
from jax import lax
from jax.experimental import pallas as pl
from jax.experimental.pallas import tpu as pltpu
from jax.sharding import PartitionSpec as P

HEAD_DIM = 64
NORM_EPS = 1e-05
ROPE_BASE = 160000.0
BIG = 1e30
LANES = 128
WAYS = 4
BF = jnp.bfloat16
F32 = jnp.float32
VMEM_LIMIT = 56 * 1024 * 1024


def dot_nn(a, b):
    return lax.dot_general(a, b, (((1,), (0,)), ((), ())), preferred_element_type=F32)


def dot_nt(a, b):
    return lax.dot_general(a, b, (((1,), (1,)), ((), ())), preferred_element_type=F32)


def dot_tn(a, b):
    return lax.dot_general(a, b, (((0,), (0,)), ((), ())), preferred_element_type=F32)


def norm_stats(values):
    centre = jnp.mean(values, axis=-1, keepdims=True)
    shifted = values - centre
    spread = jnp.mean(shifted * shifted, axis=-1, keepdims=True)
    scale = lax.rsqrt(spread + NORM_EPS)
    return shifted * scale, scale


def norm_back(vhat, scale, gain, grad):
    u = grad * gain
    mean_u = jnp.mean(u, axis=-1, keepdims=True)
    mean_uv = jnp.mean(u * vhat, axis=-1, keepdims=True)
    return scale * (u - mean_u - vhat * mean_uv)


def doc_positions(segment):
    length = segment.shape[0]
    places = jnp.arange(length, dtype=jnp.int32)
    before = jnp.concatenate([jnp.full((1,), -1, jnp.int32), segment[:-1]])
    starts = jnp.where(segment != before, places, jnp.zeros_like(places))
    return places - lax.cummax(starts, axis=0)


def rope_tables(positions):
    half = HEAD_DIM // 2
    lane = jnp.arange(LANES, dtype=jnp.int32)
    frequency = jnp.exp((lane % half).astype(F32) * (-2.0 * math.log(ROPE_BASE) / HEAD_DIM))
    angle = positions.astype(F32)[:, None] * frequency[None, :]
    first = (lane % HEAD_DIM < half)[None, :]
    sine = jnp.sin(angle)
    return jnp.cos(angle), jnp.where(first, -sine, sine)


def swap_halves(values):
    lane = lax.broadcasted_iota(jnp.int32, values.shape, 1)
    first = lane % HEAD_DIM < HEAD_DIM // 2
    back = pltpu.roll(values, LANES - HEAD_DIM // 2, 1)
    ahead = pltpu.roll(values, HEAD_DIM // 2, 1)
    return jnp.where(first, back, ahead)


def choose(at, values):
    out = values[0]
    for i in range(1, len(values)):
        out = jnp.where(at == i, values[i], out)
    return out


def params():
    return pltpu.CompilerParams(vmem_limit_bytes=VMEM_LIMIT)


def cost(flops, mib):
    return pl.CostEstimate(flops=int(flops), bytes_accessed=int(mib * 2**20), transcendentals=0)


def call(kernel, scalars, grid, in_specs, out_specs, out_shape, scratch, estimate, name):
    spec = pltpu.PrefetchScalarGridSpec(
        num_scalar_prefetch=1,
        grid=grid,
        in_specs=in_specs,
        out_specs=out_specs,
        scratch_shapes=scratch,
    )
    return functools.partial(
        pl.pallas_call(
            kernel,
            grid_spec=spec,
            out_shape=out_shape,
            compiler_params=params(),
            cost_estimate=estimate,
            name=name,
        ),
        scalars,
    )


def full(shape):
    return pl.BlockSpec(shape, lambda i, s: (0,) * len(shape))


def shape_of(shape, dtype):
    return jax.ShapeDtypeStruct(shape, dtype)


def side_by_side(ref, *at):
    return jnp.concatenate([ref[(d, *at)] for d in range(ref.shape[0])], axis=-1)


def qkv_kernel(s_ref, x_ref, gain_ref, w_ref, cos_ref, sin_ref, n_ref, q_ref, k_ref, v_ref):
    vhat, unused = norm_stats(x_ref[...].astype(F32))
    normed = (vhat * gain_ref[...]).astype(BF)
    n_ref[...] = normed
    flat = dot_nt(normed, side_by_side(w_ref, 0))
    cosine = cos_ref[...]
    sine = sin_ref[...]
    for pair in range(q_ref.shape[1] // LANES):
        here = slice(pair * LANES, (pair + 1) * LANES)
        for part, out in ((0, q_ref), (1, k_ref)):
            at = (pair * 3 + part) * LANES
            u = flat[:, at : at + LANES]
            out[:, here] = (u * cosine + swap_halves(u) * sine).astype(BF)
        at = (pair * 3 + 2) * LANES
        v_ref[:, here] = flat[:, at : at + LANES].astype(BF)


def qkv_call(scalars, x, gain, weight, cosine, sine):
    tokens, model = x.shape
    rows = tokens // WAYS
    wide, unused, cols3, unused = weight.shape
    cols = cols3 // 3
    block = lambda width: pl.BlockSpec((rows, width), lambda i, s: (i, 0))
    return call(
        qkv_kernel,
        scalars,
        (WAYS,),
        [
            block(model),
            full((1, model)),
            pl.BlockSpec((wide, 1, cols3, LANES), lambda i, s: (0, s[2], 0, 0)),
            block(LANES),
            block(LANES),
        ],
        [block(model)] + [block(cols)] * 3,
        [shape_of((tokens, model), BF)] + [shape_of((tokens, cols), BF)] * 3,
        [],
        cost(2 * tokens * model * cols3, 14),
        "qkv",
    )(x, gain, weight, cosine, sine)


def attn_fwd_kernel(s_ref, *refs):
    q_ref, k_ref, v_ref, qaux_ref, kaux_ref, live_ref = refs[:6]
    o_refs, qa_ref, ka_ref, s_scr = refs[6:10], refs[10], refs[11], refs[12]
    step = pl.program_id(0)
    rows = q_ref.shape[0]
    chunk = k_ref.shape[0] // WAYS
    per = chunk // rows
    piece = step // per
    lane_k = lax.broadcasted_iota(jnp.int32, (chunk, LANES), 1)
    lane = lax.broadcasted_iota(jnp.int32, (rows, LANES), 1)

    @pl.when(step == 0)
    def _():
        for m in range(WAYS):
            some = slice(m * chunk, (m + 1) * chunk)
            k = k_ref[some, :]
            kaux = kaux_ref[some, :]
            ka_ref[0, some, :] = jnp.where(lane_k < HEAD_DIM, k, kaux)
            ka_ref[1, some, :] = jnp.where(lane_k >= HEAD_DIM, k, kaux)

    q = q_ref[...] * jnp.asarray(HEAD_DIM**-0.5, BF)
    qaux = qaux_ref[...]
    live = live_ref[...]
    outs = []
    for head in range(2):
        mine = (lane < HEAD_DIM) if head == 0 else (lane >= HEAD_DIM)
        qa = jnp.where(mine, q, qaux)
        top = None
        for m in range(WAYS):
            some = slice(m * chunk, (m + 1) * chunk)
            s = dot_nt(qa, ka_ref[head, some, :])
            s_scr[:, some] = s
            part = jnp.max(s, axis=-1, keepdims=True)
            top = part if top is None else jnp.maximum(top, part)
        total = jnp.zeros((rows, 1), F32)
        mixed = jnp.zeros((rows, LANES), F32)
        for m in range(WAYS):
            p = jnp.exp(s_scr[:, m * chunk : (m + 1) * chunk] - top)
            total += jnp.sum(p, axis=-1, keepdims=True)
            mixed += dot_nn(p.astype(BF), v_ref[m * chunk : (m + 1) * chunk, :])
        outs.append(mixed * (live / total))
        log_sum = jnp.where(live > 0, top + jnp.log(total), BIG)
        high = log_sum.astype(BF)
        rest = log_sum - high.astype(F32)
        mid = rest.astype(BF)
        low = (rest - mid.astype(F32)).astype(BF)
        t = lane % HEAD_DIM
        aux = jnp.where(t == 16, -high, jnp.where(t == 17, -mid, jnp.where(t == 18, -low, qaux)))
        qa_ref[head] = jnp.where(mine, q, aux)
    out = jnp.where(lane < HEAD_DIM, outs[0], outs[1]).astype(BF)
    for m in range(WAYS):

        @pl.when(piece == m)
        def _(m=m):
            o_refs[m][...] = out


def piece_block(m, rows, per):
    return pl.BlockSpec((rows, LANES), lambda i, s: (jnp.clip(i - per * m, 0, per - 1), 0))


def attn_fwd_call(scalars, q, k, v, qaux, kaux, live, pair):
    tokens = q.shape[0]
    chunk = tokens // WAYS
    rows = 256
    per = chunk // rows
    fixed = pl.BlockSpec((tokens, LANES), lambda i, s: (0, pair))
    block = pl.BlockSpec((rows, LANES), lambda i, s: (i, 0))
    outs = call(
        attn_fwd_kernel,
        scalars,
        (tokens // rows,),
        [
            pl.BlockSpec((rows, LANES), lambda i, s: (i, pair)),
            fixed,
            fixed,
            block,
            full((tokens, LANES)),
            pl.BlockSpec((rows, 1), lambda i, s: (i, 0)),
        ],
        [piece_block(m, rows, per) for m in range(WAYS)]
        + [pl.BlockSpec((2, rows, LANES), lambda i, s: (0, i, 0)), full((2, tokens, LANES))],
        [shape_of((chunk, LANES), BF)] * WAYS + [shape_of((2, tokens, LANES), BF)] * 2,
        [pltpu.VMEM((rows, tokens), F32)],
        cost(16 * tokens * tokens * LANES, 4),
        "attn_fwd",
    )(q, k, v, qaux, kaux, live)
    return outs[:WAYS], outs[WAYS], outs[WAYS + 1]


def attn_bwd_kernel(s_ref, *refs):
    qa_ref, ka_ref = refs[:2]
    v_ref, do_refs, o_refs = refs[2], refs[3:7], refs[7:11]
    cosq_ref, sinq_ref, cosk_ref, sink_ref = refs[11:15]
    out_refs = refs[15:19]
    va_ref, kt_ref, dk_acc, dv_acc = refs[19:23]
    step = pl.program_id(0)
    rows = do_refs[0].shape[0]
    chunk = v_ref.shape[0] // WAYS
    per = chunk // rows
    piece = step // per
    lane_k = lax.broadcasted_iota(jnp.int32, (chunk, LANES), 1)
    lane = lax.broadcasted_iota(jnp.int32, (rows, LANES), 1)
    zero = jnp.zeros((), BF)

    @pl.when(step == 0)
    def _():
        ones = jnp.where(lane_k % HEAD_DIM < 3, jnp.ones((), BF), zero)
        for m in range(WAYS):
            some = slice(m * chunk, (m + 1) * chunk)
            v = v_ref[some, :]
            for head in range(2):
                mine = (lane_k < HEAD_DIM) if head == 0 else (lane_k >= HEAD_DIM)
                va_ref[head, some, :] = jnp.where(mine, v, ones)
                own = jnp.where(mine, ka_ref[head, some, :], zero).astype(F32)
                kt_ref[head, :, some] = own.T.astype(BF)
        dk_acc[...] = jnp.zeros_like(dk_acc)
        dv_acc[...] = jnp.zeros_like(dv_acc)

    grad = choose(piece, [r[...] for r in do_refs])
    out = choose(piece, [r[...] for r in o_refs])
    product = grad.astype(F32) * out.astype(F32)
    turned = jnp.zeros((LANES, rows), F32)
    for head in range(2):
        mine = (lane < HEAD_DIM) if head == 0 else (lane >= HEAD_DIM)
        delta = jnp.sum(jnp.where(mine, product, 0.0), axis=-1, keepdims=True)
        high = delta.astype(BF)
        rest = delta - high.astype(F32)
        mid = rest.astype(BF)
        low = (rest - mid.astype(F32)).astype(BF)
        t = lane % HEAD_DIM
        aux = jnp.where(t == 0, -high, jnp.where(t == 1, -mid, jnp.where(t == 2, -low, zero)))
        grad_aug = jnp.where(mine, grad, aux)
        grad_own = jnp.where(mine, grad, zero)
        qa = qa_ref[head]
        q_own = jnp.where(mine, qa, zero)
        for m in range(WAYS):
            some = slice(m * chunk, (m + 1) * chunk)
            prob = jnp.exp(dot_nt(ka_ref[head, some, :], qa))
            back = dot_nt(va_ref[head, some, :], grad_aug)
            score_grad = (prob * back).astype(BF)
            dv_acc[some, :] += dot_nn(prob.astype(BF), grad_own)
            dk_acc[some, :] += dot_nn(score_grad, q_own)
            turned += dot_nn(kt_ref[head, :, some], score_grad)
    dq = turned.T * (HEAD_DIM**-0.5)
    dq = (dq * cosq_ref[...] - swap_halves(dq) * sinq_ref[...]).astype(BF)
    for m in range(WAYS):

        @pl.when(piece == m)
        def _(m=m):
            here = pl.ds(pl.multiple_of((step - m * per) * rows, rows), rows)
            out_refs[m][here, :LANES] = dq

    @pl.when(step == pl.num_programs(0) - 1)
    def _():
        for m in range(WAYS):
            some = slice(m * chunk, (m + 1) * chunk)
            dk = dk_acc[some, :]
            dk = dk * cosk_ref[some, :] - swap_halves(dk) * sink_ref[some, :]
            out_refs[m][:, LANES : 2 * LANES] = dk.astype(BF)
            out_refs[m][:, 2 * LANES :] = dv_acc[some, :].astype(BF)


def attn_bwd_call(scalars, qa, ka, v, grad, o, cosine, sine, pair):
    tokens = v.shape[0]
    chunk = tokens // WAYS
    rows = 256
    per = chunk // rows
    moving = [piece_block(m, rows, per) for m in range(WAYS)]
    block = pl.BlockSpec((rows, LANES), lambda i, s: (i, 0))
    return call(
        attn_bwd_kernel,
        scalars,
        (tokens // rows,),
        [pl.BlockSpec((2, rows, LANES), lambda i, s: (0, i, 0)), full((2, tokens, LANES))]
        + [pl.BlockSpec((tokens, LANES), lambda i, s: (0, pair))]
        + moving * 2
        + [block, block, full((tokens, LANES)), full((tokens, LANES))],
        [full((chunk, 3 * LANES))] * WAYS,
        [shape_of((chunk, 3 * LANES), BF)] * WAYS,
        [
            pltpu.VMEM((2, tokens, LANES), BF),
            pltpu.VMEM((2, LANES, tokens), BF),
            pltpu.VMEM((tokens, LANES), F32),
            pltpu.VMEM((tokens, LANES), F32),
        ],
        cost(28 * tokens * tokens * LANES, 8),
        "attn_bwd",
    )(qa, ka, v, *grad, *o, cosine, sine, cosine, sine)


def middle_kernel(s_ref, *refs):
    o_refs = refs[:8]
    x_ref, w_ref, gain_ref, live_ref, middle_ref, inner_ref, square_ref = refs[8:]
    z = s_ref[0]
    tokens = x_ref[...].astype(F32)
    attn_out = jnp.zeros(tokens.shape, F32)
    for m in range(WAYS):
        o = jnp.concatenate([o_refs[2 * m][...], o_refs[2 * m + 1][...]], axis=-1)
        attn_out += dot_nn(o, side_by_side(w_ref, z ^ m))
    middle = tokens + attn_out
    vhat, unused = norm_stats(middle)
    middle_ref[...] = middle
    inner_ref[...] = (vhat * gain_ref[...]).astype(BF)
    live = live_ref[...]
    square_ref[...] = jnp.concatenate(
        [jnp.sum(live * a * a, axis=0, keepdims=True) for a in (tokens, attn_out, middle)]
        + [jnp.zeros((5, tokens.shape[1]), F32)],
        axis=0,
    )


def middle_call(scalars, heads, x, weight, gain, live):
    rows, model = x.shape
    wide = weight.shape[0]
    depth = model // WAYS
    return call(
        middle_kernel,
        scalars,
        (1,),
        [full((rows, LANES))] * 8
        + [
            full((rows, model)),
            full((wide, WAYS, depth, LANES)),
            full((1, model)),
            full((rows, 1)),
        ],
        [full((rows, model)), full((rows, model)), full((8, model))],
        [shape_of((rows, model), F32), shape_of((rows, model), BF), shape_of((8, model), F32)],
        [],
        cost(2 * rows * model * model, 8),
        "middle",
    )(*heads, x, weight, gain, live)


def middle_back_kernel(
    s_ref, middle_ref, mlp_ref, back_ref, grad_ref, w_ref, gain_ref, live_ref,
    output_ref, mgrad_ref, low_ref, small_ref, *hg_refs,
):
    z = s_ref[0]
    middle = middle_ref[...]
    mlp = mlp_ref[...]
    back = back_ref[...]
    vhat, scale = norm_stats(middle)
    middle_grad = grad_ref[...].astype(F32) + norm_back(vhat, scale, gain_ref[...], back)
    low = middle_grad.astype(BF)
    for m in range(WAYS):
        hg = dot_nt(low, side_by_side(w_ref, z ^ m)).astype(BF)
        hg_refs[2 * m][...] = hg[:, :LANES]
        hg_refs[2 * m + 1][...] = hg[:, LANES:]
    mgrad_ref[...] = middle_grad
    low_ref[...] = low
    output_ref[...] = (middle + mlp).astype(BF)
    small_ref[...] = jnp.concatenate(
        [
            jnp.sum(live_ref[...] * mlp * mlp, axis=0, keepdims=True),
            jnp.sum(back * vhat, axis=0, keepdims=True),
            jnp.zeros((6, mlp.shape[1]), F32),
        ],
        axis=0,
    )


def middle_back_call(scalars, middle, mlp, back, grad, weight, gain, live):
    rows, model = middle.shape
    wide = weight.shape[0]
    depth = model // WAYS
    outs = call(
        middle_back_kernel,
        scalars,
        (1,),
        [full((rows, model))] * 4
        + [full((wide, WAYS, depth, LANES)), full((1, model)), full((rows, 1))],
        [full((rows, model))] * 3 + [full((8, model))] + [full((rows, LANES))] * 8,
        [
            shape_of((rows, model), BF),
            shape_of((rows, model), F32),
            shape_of((rows, model), BF),
            shape_of((8, model), F32),
        ]
        + [shape_of((rows, LANES), BF)] * 8,
        [],
        cost(2 * rows * model * model, 12),
        "middle_back",
    )(middle, mlp, back, grad, weight, gain, live)
    return outs[:4], outs[4:]


def own_first(core, values):
    cut = [values[:, at : at + LANES] for at in range(0, values.shape[1], LANES)]
    turned = [cut[i ^ 1] for i in range(len(cut))]
    return jnp.where(core == 0, values, jnp.concatenate(turned, axis=-1))


def put_slabs(keep_ref, send_ref, value, *at):
    for d in range(value.shape[1] // LANES):
        ref = send_ref if d % 2 else keep_ref
        ref[(d // 2, *at)] = value[:, d * LANES : (d + 1) * LANES]


def attn_grad_kernel(s_ref, *refs):
    o_refs, low_ref, keep_ref, send_ref = refs[:8], refs[8], refs[9], refs[10]
    low = own_first(s_ref[1], low_ref[...])
    for m in range(WAYS):
        o = jnp.concatenate([o_refs[2 * m][...], o_refs[2 * m + 1][...]], axis=-1)
        put_slabs(keep_ref, send_ref, dot_tn(o, low).astype(BF), s_ref[0] ^ m)


def attn_grad_call(scalars, heads, low):
    rows, model = low.shape
    shape = (model // LANES // 2, WAYS, model // WAYS, LANES)
    return call(
        attn_grad_kernel,
        scalars,
        (1,),
        [full((rows, LANES))] * 8 + [full((rows, model))],
        [full(shape)] * 2,
        [shape_of(shape, BF)] * 2,
        [],
        cost(2 * rows * model * model, 6),
        "attn_grad",
    )(*heads, low)


def ffn_kernel(s_ref, x_ref, g_ref, wa_ref, wb_ref, mlp_ref, back_ref, keep_ref, send_ref):
    step = pl.program_id(0)
    units = wb_ref.shape[2] // 2
    skip = wa_ref.shape[2] - units
    w_act = side_by_side(wa_ref, 0, slice(skip, skip + units))
    w_lin = side_by_side(wb_ref, 0, slice(0, units))
    w_out = side_by_side(wb_ref, 0, slice(units, 2 * units))
    x = x_ref[...]
    grad = g_ref[...]
    act_in = dot_nt(w_act, x)
    linear = dot_nt(w_lin, x)
    hidden_grad = dot_nt(w_out, grad)
    cdf = 0.5 * (1.0 + lax.erf(act_in * (2.0**-0.5)))
    act = act_in * cdf
    slope = cdf + act_in * jnp.exp(-0.5 * act_in * act_in) * ((2.0 * math.pi) ** -0.5)
    hidden = (act * linear).astype(BF)
    d_act = (hidden_grad * linear * slope).astype(BF)
    d_lin = (hidden_grad * act).astype(BF)
    x = own_first(s_ref[1], x)
    grad = own_first(s_ref[1], grad)
    for part, value in ((0, dot_nn(d_act, x)), (1, dot_nn(d_lin, x)), (2, dot_nn(hidden, grad))):
        some = slice(part * units, (part + 1) * units)
        put_slabs(keep_ref, send_ref, value.astype(BF), 0, some)
    mlp = dot_tn(hidden, w_out)
    back = dot_tn(d_act, w_act) + dot_tn(d_lin, w_lin)

    @pl.when(step == 0)
    def _():
        mlp_ref[...] = mlp
        back_ref[...] = back

    @pl.when(step > 0)
    def _():
        mlp_ref[...] += mlp
        back_ref[...] += back


def ffn_call(scalars, x, grad, pack_a, pack_b):
    tokens, model = x.shape
    wide, quarters, depth_a, unused = pack_a.shape
    depth_b = pack_b.shape[2]
    units = depth_b // 2
    out = (wide // 2, quarters, 3 * units, LANES)
    part = pl.BlockSpec((wide // 2, 1, 3 * units, LANES), lambda i, s: (0, i, 0, 0))
    weight = lambda depth: pl.BlockSpec((wide, 1, depth, LANES), lambda i, s: (0, i, 0, 0))
    return call(
        ffn_kernel,
        scalars,
        (quarters,),
        [full((tokens, model))] * 2 + [weight(depth_a), weight(depth_b)],
        [full((tokens, model))] * 2 + [part] * 2,
        [shape_of((tokens, model), F32)] * 2 + [shape_of(out, BF)] * 2,
        [],
        cost(18 * tokens * model * units * quarters, 40),
        "ffn",
    )(x, grad, pack_a, pack_b)


def qkv_grad_kernel(s_ref, *refs):
    low_refs, normed_ref, keep_ref, send_ref = refs[:4], refs[4], refs[5], refs[6]
    rows = low_refs[0].shape[0]
    total = None
    for m in range(WAYS):
        part = dot_tn(low_refs[m][...], normed_ref[m * rows : (m + 1) * rows, :])
        total = part if total is None else total + part
    value = total.astype(BF)
    for d in range(value.shape[1] // LANES):
        slab = value[:, d * LANES : (d + 1) * LANES]
        x = (d // 2) % 2
        at = d // 4 * 2 + d % 2

        @pl.when(s_ref[3] == x)
        def _():
            keep_ref[at] = slab

        @pl.when(s_ref[3] != x)
        def _():
            send_ref[at] = slab


def qkv_grad_call(scalars, low, normed):
    tokens, model = normed.shape
    rows, cols = low[0].shape
    shape = (model // LANES // 2, cols, LANES)
    return call(
        qkv_grad_kernel,
        scalars,
        (1,),
        [full((rows, cols))] * WAYS + [full((tokens, model))],
        [full(shape)] * 2,
        [shape_of(shape, BF)] * 2,
        [],
        cost(2 * WAYS * rows * model * cols, 7),
        "qkv_grad",
    )(*low, normed)


def input_grad_kernel(s_ref, *refs):
    low_refs = refs[:8]
    w_ref, x_ref, mgrad_ref, gain_ref, grad_ref, gain_part_ref = refs[8:]
    z = s_ref[0]
    normed_grad = jnp.zeros(x_ref.shape, F32)
    for m in range(WAYS):
        w = side_by_side(w_ref, z ^ m)
        for pair in range(2):
            at = pair * 3 * LANES
            normed_grad += dot_nn(low_refs[2 * m + pair][...], w[at : at + 3 * LANES, :])
    vhat, scale = norm_stats(x_ref[...].astype(F32))
    gain_part_ref[...] = jnp.sum(normed_grad * vhat, axis=0, keepdims=True)
    grad_ref[...] = mgrad_ref[...] + norm_back(vhat, scale, gain_ref[...], normed_grad)


def input_grad_call(scalars, low, weight, x, middle_grad, gain):
    rows, model = x.shape
    return call(
        input_grad_kernel,
        scalars,
        (1,),
        [full((rows, 3 * LANES))] * 8
        + [full(weight.shape), full((rows, model)), full((rows, model)), full((1, model))],
        [full((rows, model)), full((1, model))],
        [shape_of((rows, model), F32), shape_of((1, model), F32)],
        [],
        cost(6 * rows * model * model, 14),
        "input_grad",
    )(*low, weight, x, middle_grad, gain)


MESH = pl.DeviceIdType.MESH
UP, DOWN, TO_X, TO_Y, TO_D, CORE_OWN, CORE_X, CORE_Y, CORE_D = range(9)
FROM_Z, FROM_X, FROM_Y, FROM_D = range(4)


def gather_kernel(x_ref, *refs, packs):
    parts, x_all, outs = refs[:packs], refs[packs], refs[packs + 1 : 2 * packs + 1]
    sends, recvs, cores, locals_, token_send, token_recv = refs[2 * packs + 1 :]
    dp, z = lax.axis_index("dp"), lax.axis_index("mp")
    core, xb, yb = dp % 2, (dp // 2) % 2, dp // 4
    at_c, at_x, at_y = dp + 1 - 2 * core, dp + 2 - 4 * xb, dp + 4 - 8 * yb
    at_d = at_x + at_y - dp
    group = z // 2
    quarter = z + 2 * core - 4 * core * group

    def flip1(q):
        return q + 1 - 2 * (q % 2)

    def attention_of(m):
        h = z if m == 0 else flip1(z)
        a, g = h // 2, core
        return dp - core + a + g - 2 * a * g, 2 * core + h % 2

    def owner_of(m):
        return dp - core + group, (quarter if m == 0 else flip1(quarter))

    barrier = pltpu.get_barrier_semaphore()

    def greet(device, when=None):
        def signal():
            pl.semaphore_signal(barrier, inc=1, device_id=device, device_id_type=MESH)

        signal() if when is None else pl.when(when)(signal)

    greet((at_c, z))
    greet((at_x, z))
    greet((at_y, z))
    greet((dp, z + 1), z < WAYS - 1)
    greet((dp, z - 1), z > 0)
    here = []
    for m in range(2):
        to_dp, to_z = attention_of(m)
        from_dp, from_z = owner_of(m)
        stays = jnp.logical_and(to_dp == dp, to_z == z)
        here.append((to_dp, to_z, stays))
        greet((from_dp, from_z), jnp.logical_not(jnp.logical_and(from_dp == dp, from_z == z)))
    count = 3 + (z < WAYS - 1).astype(jnp.int32) + (z > 0).astype(jnp.int32)
    for m in range(2):
        count += 1 - here[m][2].astype(jnp.int32)
    pl.semaphore_wait(barrier, count)

    def remote(src, dst, send, recv, device):
        return pltpu.make_async_remote_copy(
            src_ref=src, dst_ref=dst, send_sem=send, recv_sem=recv,
            device_id=device, device_id_type=MESH,
        )

    def copy(p, kind, s, src=None):
        who = {CORE_X: at_x, CORE_Y: at_y, CORE_D: at_d}.get(kind, dp)
        if kind == TO_D:
            who = jnp.where(s < 2, at_x, at_y)
        slab = outs[p].at[who, s]
        send = sends.at[p, kind, s]
        if kind == UP:
            recv, device = recvs.at[p, FROM_Z, s], (dp, z + 1)
        elif kind == DOWN:
            recv, device = recvs.at[p, FROM_Z, s], (dp, z - 1)
        elif kind == TO_X:
            recv, device = recvs.at[p, FROM_X, s], (at_x, z)
        elif kind == TO_Y:
            recv, device = recvs.at[p, FROM_Y, s], (at_y, z)
        elif kind == TO_D:
            recv, device = recvs.at[p, FROM_D, s], (jnp.where(s < 2, at_y, at_x), z)
        else:
            recv, device = cores.at[p, kind - CORE_OWN, s], (at_c, z)
        return remote(slab if src is None else src, slab, send, recv, device)

    def arrived(p, sem, who, s):
        slab = outs[p].at[who, s]
        remote(slab, slab, sends.at[p, UP, s], sem, (at_c, z)).wait_recv()

    def spread(p, s, src=None):
        copy(p, TO_X, s, src).start()
        copy(p, TO_Y, s, src).start()
        copy(p, CORE_OWN, s, src).start()

    def begin(p):
        src = parts[p]
        pl.when(z < WAYS - 1)(lambda: copy(p, UP, z, src).start())
        pl.when(z > 0)(lambda: copy(p, DOWN, z, src).start())
        spread(p, z, src)
        pltpu.make_async_copy(src, outs[p].at[dp, z], locals_.at[p]).start()

    def line(p, hop):
        def below():
            s = z - hop
            arrived(p, recvs.at[p, FROM_Z, s], dp, s)
            pl.when(z < WAYS - 1)(lambda: copy(p, UP, s).start())
            spread(p, s)

        def above():
            s = z + hop
            arrived(p, recvs.at[p, FROM_Z, s], dp, s)
            pl.when(z > 0)(lambda: copy(p, DOWN, s).start())
            spread(p, s)

        pl.when(z >= hop)(below)
        pl.when(z + hop < WAYS)(above)

    def plane(p, hop):
        def one(s):
            arrived(p, recvs.at[p, FROM_X, s], at_x, s)
            copy(p, CORE_X, s).start()
            pl.when(s < 2)(lambda: copy(p, TO_D, s).start())
            arrived(p, recvs.at[p, FROM_Y, s], at_y, s)
            copy(p, CORE_Y, s).start()
            pl.when(s >= 2)(lambda: copy(p, TO_D, s).start())

        if hop == 0:
            one(z)
        else:
            pl.when(z >= hop)(lambda: one(z - hop))
            pl.when(z + hop < WAYS)(lambda: one(z + hop))

    def corner(p, hop):
        def one(s):
            arrived(p, recvs.at[p, FROM_D, s], at_d, s)
            copy(p, CORE_D, s).start()

        if hop == 0:
            one(z)
        else:
            pl.when(z >= hop)(lambda: one(z - hop))
            pl.when(z + hop < WAYS)(lambda: one(z + hop))

    def finish(p):
        for s in range(WAYS):
            for kind in range(4):
                twin = (at_c, at_x + at_c - dp, at_y + at_c - dp, at_d + at_c - dp)[kind]
                arrived(p, cores.at[p, kind, s], twin, s)
        pltpu.make_async_copy(parts[p], outs[p].at[dp, z], locals_.at[p]).wait()
        for s in range(WAYS):
            pl.when(jnp.logical_and(z < WAYS - 1, s <= z))(lambda s=s: copy(p, UP, s).wait_send())
            pl.when(jnp.logical_and(z > 0, s >= z))(lambda s=s: copy(p, DOWN, s).wait_send())
            for kind in range(TO_X, CORE_D + 1):
                copy(p, kind, s).wait_send()

    def token(m):
        to_dp, to_z, stays = here[m]
        far = remote(x_ref, x_all.at[m], token_send.at[m], token_recv.at[m], (to_dp, to_z))
        near = pltpu.make_async_copy(x_ref, x_all.at[m], token_recv.at[m])
        return far, near, stays

    def pass_on(m):
        return remote(
            x_all.at[m], x_all.at[m + 2], token_send.at[m + 2], token_recv.at[m + 2], (at_c, z)
        )

    begin(0)
    for m in range(2):
        far, near, stays = token(m)
        pl.when(stays)(near.start)
        pl.when(jnp.logical_not(stays))(far.start)
    for p in range(1, packs):
        begin(p)
    for hop in range(1, WAYS):
        line(0, hop)
    for hop in range(WAYS):
        plane(0, hop)
    for m in range(2):
        token(m)[0].wait_recv()
        pass_on(m).start()
    for hop in range(WAYS):
        corner(0, hop)
    for p in range(1, packs):
        for hop in range(1, WAYS):
            line(p, hop)
        for hop in range(WAYS):
            plane(p, hop)
        for hop in range(WAYS):
            corner(p, hop)
    for m in range(2):
        pass_on(m).wait()
        far, near, stays = token(m)
        pl.when(jnp.logical_not(stays))(far.wait_send)
    for p in range(packs):
        finish(p)


def gather_call(x, parts, dps):
    rows, model = x.shape
    packs = len(parts)
    anywhere = pl.BlockSpec(memory_space=pl.ANY)
    out = pl.pallas_call(
        functools.partial(gather_kernel, packs=packs),
        in_specs=[anywhere] * (1 + packs),
        out_specs=[anywhere] * (1 + packs),
        out_shape=[shape_of((WAYS, rows, model), BF)]
        + [shape_of((dps, WAYS) + part.shape, BF) for part in parts],
        scratch_shapes=[
            pltpu.SemaphoreType.DMA((packs, 9, WAYS)),
            pltpu.SemaphoreType.DMA((packs, 4, WAYS)),
            pltpu.SemaphoreType.DMA((packs, 4, WAYS)),
            pltpu.SemaphoreType.DMA((packs,)),
            pltpu.SemaphoreType.DMA((WAYS,)),
            pltpu.SemaphoreType.DMA((WAYS,)),
        ],
        compiler_params=pltpu.CompilerParams(collective_id=0, has_side_effects=True),
        name="gather",
    )(x, *parts)
    return out[0].reshape(WAYS * rows, model), out[1:]


def after(value, *others):
    return lax.optimization_barrier((value, *others))[0]


def add_low(a, b):
    return (a.astype(F32) + b.astype(F32)).astype(BF)


def pick(values, at, axis=0):
    return lax.dynamic_index_in_dim(values, at, axis, keepdims=False)


def flip(values, bit, dps):
    return lax.ppermute(values, "dp", [(i, i ^ bit) for i in range(dps)])


def to_attention(values, m, dps, back=False):
    pairs = []
    for dp in range(dps):
        group = dp % 2
        for t in range(WAYS):
            quarter = t ^ m
            there = (dp - group + ((quarter // 2) ^ group)) * WAYS + 2 * group + quarter % 2
            pairs.append((there, dp * WAYS + t) if back else (dp * WAYS + t, there))
    return lax.ppermute(values, ("dp", "mp"), pairs)


class Sum:
    def __init__(self, keep, send, place):
        self.place = place
        self.keep = keep.reshape((2, 2) + keep.shape[1:])
        self.got = flip(send, 1, 8).reshape(self.keep.shape)

    def planes(self):
        core, x, y, me = self.place
        half = self.keep.shape[2] // 2
        a = [v[:, :, :half] for v in (self.keep, self.got)]
        b = [v[:, :, half:] for v in (self.keep, self.got)]
        self.a = add_low(pick(a[0], x, 1), pick(a[1], x, 1))
        self.b = add_low(pick(b[0], y, 0), pick(b[1], y, 0))
        send_a = add_low(pick(a[0], 1 - x, 1), pick(a[1], 1 - x, 1))
        send_b = add_low(pick(b[0], 1 - y, 0), pick(b[1], 1 - y, 0))
        self.got_a = flip(send_a, 2, 8)
        self.got_b = flip(send_b, 4, 8)
        return send_a, send_b

    def planes_again(self):
        core, x, y, me = self.place
        send_a = add_low(pick(self.a, 1 - y), pick(self.got_a, 1 - y))
        send_b = add_low(pick(self.b, 1 - x), pick(self.got_b, 1 - x))
        self.a = add_low(pick(self.a, y), pick(self.got_a, y))
        self.b = add_low(pick(self.b, x), pick(self.got_b, x))
        self.got_a = flip(send_a, 4, 8)
        self.got_b = flip(send_b, 2, 8)
        return send_a, send_b

    def line(self):
        core, x, y, me = self.place
        g = jnp.concatenate([add_low(self.a, self.got_a), add_low(self.b, self.got_b)], axis=0)
        sent = [pick(g, (me + k) % WAYS) for k in range(1, WAYS)]
        self.own = pick(g, me)
        self.parts = [
            lax.ppermute(sent[k - 1], "mp", [(i, (i + k) % WAYS) for i in range(WAYS)])
            for k in range(1, WAYS)
        ]
        return tuple(sent)

    def total(self):
        out = self.own.astype(F32)
        for part in self.parts:
            out += part.astype(F32)
        return out


def sum_small(values, sizes):
    for axis, size in sizes:
        total = values
        for k in range(1, size):
            total += lax.ppermute(values, axis, [(i, (i + k) % size) for i in range(size)])
        values = total
    return values


def local(
    sizes,
    layer_input,
    segment_ids,
    grad_out,
    qkv_weight,
    attn_weight,
    inner_weight,
    outer_weight,
    attn_gain,
    mlp_gain,
):
    dps, mps = sizes
    rows, model = layer_input.shape
    head_cols = qkv_weight.shape[2]
    units = inner_weight.shape[2]
    pairs = head_cols // LANES
    wide = model // LANES
    special = dps == wide
    me = lax.axis_index("mp")
    dp = lax.axis_index("dp")
    core, x_at, y_at = dp % 2, (dp // 2) % 2, dp // 4
    group = me // 2
    quarter = me ^ (2 * core)
    scalars = jnp.stack([me, core, quarter, x_at]).astype(jnp.int32)
    place = (core, x_at, y_at, me)

    def every(values):
        got = lax.all_gather(values, ("dp", "mp"), axis=0)
        if not special:
            ratio = dps // wide
            got = got.reshape((wide, ratio, mps) + values.shape)
            return jnp.moveaxis(got, 1, -2).reshape((wide, mps, values.shape[0], LANES))
        return got.reshape((dps, mps) + values.shape)

    qkv_part = qkv_weight.transpose(1, 2, 0).reshape(3, pairs, LANES, -1)
    qkv_part = qkv_part.transpose(1, 0, 2, 3).reshape(3 * head_cols, -1)
    inner_t = inner_weight.transpose(1, 2, 0)
    outer_t = outer_weight.T
    attn_depth = model // mps
    part_a = jnp.concatenate([attn_weight.T, inner_t[0]], axis=0)
    part_b = jnp.concatenate([inner_t[1], outer_t], axis=0)
    if special:
        x_all, (qkv_all, pack_a, pack_b) = gather_call(layer_input, [qkv_part, part_a, part_b], dps)
    else:
        x_pieces = [to_attention(layer_input, m, dps) for m in range(WAYS)]
        x_all = jnp.concatenate(x_pieces, axis=0)
        qkv_all, pack_a, pack_b = every(qkv_part), every(part_a), every(part_b)

    mine = segment_ids[0]
    other = flip(mine, 1, dps)
    segment = jnp.where(group == core, mine, other)
    order = [pick(segment.reshape(WAYS, rows), quarter ^ m) for m in range(WAYS)]
    positions = doc_positions(segment).reshape(WAYS, rows)
    positions = jnp.concatenate([pick(positions, quarter ^ m) for m in range(WAYS)])
    segment = jnp.concatenate(order)
    cosine, sine = rope_tables(positions)
    lane = jnp.arange(LANES, dtype=jnp.int32) % HEAD_DIM
    same = segment[:, None] == lane[None, :]
    qaux = jnp.where(same | (lane >= 16)[None, :], 0.0, -BIG).astype(BF)
    kaux = jnp.where(same & (lane < 16)[None, :], 1.0, 0.0)
    kaux = jnp.where(((lane >= 16) & (lane < 19))[None, :], 1.0, kaux).astype(BF)
    live = (segment != 0).astype(F32)[:, None]
    live_mine = (pick(mine.reshape(WAYS, rows), me) != 0).astype(F32)[:, None]

    normed, q, k, v = qkv_call(scalars, x_all, attn_gain[None], qkv_all, cosine, sine)

    kept, heads = [], [None] * (2 * WAYS)
    for pair in range(pairs):
        o, qa, ka = attn_fwd_call(scalars, q, k, v, qaux, kaux, live, pair)
        kept.append((o, qa, ka))
        for m in range(WAYS):
            heads[2 * m + pair] = to_attention(o[m], m, dps, back=True)
    middle, inner_in, squares = middle_call(
        scalars, heads, layer_input, pack_a, mlp_gain[None], live_mine
    )
    mlp_out, inner_back, keep_f, send_f = ffn_call(scalars, inner_in, grad_out, pack_a, pack_b)
    if special:
        sum_f = Sum(keep_f, send_f, place)
    (layer_output, middle_grad, middle_low, small), heads_grad = middle_back_call(
        scalars, middle, mlp_out, inner_back, grad_out, pack_a, mlp_gain[None], live_mine
    )
    grads = [
        [to_attention(heads_grad[2 * m + pair], m, dps) for m in range(WAYS)]
        for pair in range(pairs)
    ]
    keep_c, send_c = attn_grad_call(scalars, heads, middle_low)
    if special:
        sum_c = Sum(keep_c, send_c, place)

    returned, low = [None] * (2 * WAYS), []
    qkv_sums = []
    for pair in range(pairs):
        o, qa, ka = kept[pair]
        grad = grads[pair]
        if special:
            if pair == 0:
                waits = sum_f.planes()
            else:
                waits = (*sum_f.planes_again(), *sum_c.planes())
            grad = [after(grad[0], *waits), *grad[1:]]
        parts = attn_bwd_call(scalars, qa, ka, v, grad, o, cosine, sine, pair)
        for m in range(WAYS):
            returned[2 * m + pair] = to_attention(parts[m], m, dps, back=True)
        low.append(parts)
        keep, send = qkv_grad_call(scalars, parts, normed)
        if special:
            got = flip(send, 2, 8)
            total = [v.reshape(2, 2, -1, LANES) for v in (keep, got)]
            sent = add_low(pick(total[0], 1 - y_at), pick(total[1], 1 - y_at))
            got = flip(sent, 4, 8)
            total = add_low(
                add_low(pick(total[0], y_at), pick(total[1], y_at)), got
            )
            parts = []
            for turn in range(2):
                steps = []
                for i in range(dps):
                    for z in range(mps):
                        g, h = z // 2, z ^ (2 * (i % 2))
                        there = (i - i % 2 + (g ^ turn)) * mps + h
                        steps.append((i * mps + z, there))
                parts.append(lax.ppermute(pick(total, group ^ turn), ("dp", "mp"), steps))
            qkv_sums.append(parts[0].astype(F32) + parts[1].astype(F32))
        else:
            both = [jnp.where(x_at == i, keep, send) for i in range(2)]
            both = jnp.stack([b.reshape(wide // 4, 2, -1, LANES) for b in both], axis=1)
            both = both.reshape(wide, -1, LANES)
            slot = (jnp.arange(WAYS) == quarter)[None, :, None, None]
            qkv_sums.append(jnp.where(slot, both[:, None], jnp.zeros((), BF)))

    if special:
        sum_f.line()
        sum_c.planes_again()
        sum_c.line()
        ffn_sum, attn_sum = sum_f.total(), sum_c.total()
        qkv_sum = jnp.concatenate(qkv_sums, axis=0)
    else:

        def join(keep, send):
            both = [jnp.where(core == i, keep, send) for i in range(2)]
            return jnp.stack(both, axis=1).reshape((wide,) + keep.shape[1:])

        def shared(values):
            ratio = dps // wide
            lanes = LANES // ratio
            cut = values.reshape(values.shape[:-1] + (ratio, lanes))
            cut = jnp.moveaxis(cut, -2, 1).reshape(dps * mps, -1, lanes)
            return lax.psum_scatter(
                cut.astype(F32), ("dp", "mp"), scatter_dimension=0, tiled=True
            )[0]

        ffn_sum = shared(join(keep_f, send_f))
        attn_sum = shared(join(keep_c, send_c))
        qkv_sum = shared(jnp.concatenate(qkv_sums, axis=2))

    input_grad, attn_gain_part = input_grad_call(
        scalars, returned, qkv_all, layer_input, middle_grad, attn_gain[None]
    )

    sums = jnp.concatenate([jnp.sum(squares[:3], axis=1), jnp.sum(small[:1], axis=1)])
    sums = jnp.concatenate([sums, jnp.sum(live_mine)[None], jnp.zeros((model - 5,), F32)])
    early = jnp.stack([small[1], sums])
    if special:
        ways = (("dp", dps), ("mp", mps))
        early = sum_small(early, ways)
        attn_gain_grad = sum_small(attn_gain_part, ways)[0]
    else:
        early, attn_gain_grad = lax.psum((early, attn_gain_part[0]), ("dp", "mp"))
    rms_values = jnp.sqrt(early[1, :4] / (early[1, 4] * model))

    qkv_sum = qkv_sum.reshape(pairs, 3, LANES, -1).transpose(3, 1, 0, 2)
    ffn_sum = ffn_sum.reshape(3, units, -1)
    return (
        layer_output,
        input_grad,
        qkv_sum.reshape(-1, 3, head_cols),
        attn_sum.T,
        ffn_sum[:2].transpose(2, 0, 1),
        ffn_sum[2].T,
        attn_gain_grad,
        early[0],
        rms_values,
    )


def solution(mesh):
    sizes = (mesh.shape["dp"], mesh.shape["mp"])
    both = ("dp", "mp")
    whole = (P(both, None), P("dp", None, "mp"), P("dp", "mp"))
    return jax.shard_map(
        functools.partial(local, sizes),
        mesh=mesh,
        in_specs=(
            whole[0],
            P("dp", None),
            whole[0],
            whole[1],
            whole[2],
            whole[1],
            whole[2],
            P(),
            P(),
        ),
        out_specs=(
            whole[0],
            whole[0],
            whole[1],
            whole[2],
            whole[1],
            whole[2],
            P(),
            P(),
            P(),
        ),
        check_vma=False,
    )
```

time: 708 us -> 617 us (0.87)
  the two profiles are of different devices: /device:TPU:0 before, /device:TPU:24 now
where the time goes in v2:
time: 617 us; the launch traced here: 607 us
  Pallas kernels  339 us (55%)
  starting transfers between devices  114 us (18%)
  waiting for transfers between devices  94.2 us (15%)
  other arithmetic  37.2 us (6%)
  local copies, waits for them, and re-layouts  20.4 us (3%)
    pallas_call x1, Pallas kernels, gather_call(): pl.pallas_call(functools.partial(gather_kernel, packs=packs), in_specs=[a...  145 us
    pallas_call x2, Pallas kernels, attn_bwd_call(): call(attn_bwd_kernel, scalars, (tokens // rows,), [pl.BlockSpec((2, rows,...  61.9 us
    ppermute x24, starting transfers between devices, to_attention(): return lax.ppermute(values, ('dp', 'mp'), pairs)  52.6 us
    ppermute x6, waiting for transfers between devices, line(): lax.ppermute(sent[k - 1], 'mp', [(i, (i + k) % WAYS) for i in range(WAYS)])  40.7 us
    pallas_call x2, Pallas kernels, attn_fwd_call(): call(attn_fwd_kernel, scalars, (tokens // rows,), [pl.BlockSpec((rows, LA...  40.5 us
    pallas_call x1, Pallas kernels, ffn_call(): call(ffn_kernel, scalars, (quarters,), [full((tokens, model))] * 2 + [wei...  36.4 us
    ppermute x20, starting transfers between devices, sum_small(): lax.ppermute(values, axis, [(i, (i + k) % size) for i in range(size)])  27.8 us
    ppermute x24, waiting for transfers between devices, to_attention(): return lax.ppermute(values, ('dp', 'mp'), pairs)  25.1 us
  transfers between devices with their start and end apart: 69, of which 17 were waited for; matrix products, arithmetic and copies ran while one was open for 7% of the time, Pallas kernels for 44%

profile of v2, /device:TPU:24, one launch (start us, length us, event | category | flops | bytes accessed | tf_op | source)
XLA Modules:
  0.0 607.4 jit_solution(3630300045811511201)
XLA Ops:
  6.7 144.9 %gather.1 = (bf16[4,512,1024]{2,1,0:T(8,128)(2,1)}, bf16[8,4,768,128]{3,2,1,0:T(8,128)(2,1)}, bf16[8,4,912,128]{3,2,1,0:T(8,128)(2,1)}, bf16[8,4,1312,128]{3,2,1,0:T(8,128)(2,1)}) custom-call(bf16[512,1024]{1,0:T(8,128)(2,1)} %refs_9_.1, bf16[768,128]{1,0:T(8,128)(2,1)} %bitcast.191, bf16[912,128]{1,0:T(8,128)(2,1)} %pad_maximum_fusion.2.refs_1_, ...), custom_call_target="tpu_custom_call" | custom-call | tf_op jit(solution)/shard_map/gather/pallas_call | solution.py:810
  154.0 5.6 negate_select_fusion
  161.0 10.2 %qkv.1 = (bf16[2048,1024]{1,0:T(8,128)(2,1)}, bf16[2048,256]{1,0:T(8,128)(2,1)}, bf16[2048,256]{1,0:T(8,128)(2,1)}, bf16[2048,256]{1,0:T(8,128)(2,1)}) custom-call(s32[4]{0:T(128)} %pad_add_fusion.1.s_ref, bf16[2048,1024]{1,0:T(8,128)(2,1)} %bitcast.186, f32[1,1024]{1,0:T(1,128)} %bitcast.218, bf16[8,4,768,128]{3,2,1,0:T(8,128)(2,1)} %get-tuple-element.67.w_ref.refs_8_, ...), custom_call_target="tpu_custom_call" | custom-call | flops 3221225472 | bytes 14680064 | tf_op jit(solution)/shard_map/qkv/pallas_call | solution.py:146
  171.2 20.3 %attn_fwd.3 = (bf16[512,128]{1,0:T(8,128)(2,1)}, bf16[512,128]{1,0:T(8,128)(2,1)}, bf16[512,128]{1,0:T(8,128)(2,1)}, bf16[512,128]{1,0:T(8,128)(2,1)}, bf16[2,20...) custom-call(s32[4]{0:T(128)} %pad_add_fusion.1.s_ref, bf16[2048,256]{1,0:T(8,128)(2,1)} %get-tuple-element.68.refs_0_, ...), custom_call_target="tpu_custom_call" | custom-call | flops 8589934592 | bytes 4194304 | tf_op jit(solution)/shard_map/attn_fwd/pallas_call | solution.py:233
  193.8 7.2 %collective-permute-start.4 = (bf16[512,128]{1,0:T(8,128)(2,1)}, bf16[512,128]{1,0:T(8,128)(2,1)S(1)}, u32[]{:S(2)}, u32[]{:S(2)}) collective-permute-start(bf16[512,128]{1,0:T(8,128)(2,1)} %get-tuple-element.74.refs_8_), channel_id=1, source_target_pairs={{1,0},{0,1},{5,2},{4,3},{7,4},{6,5},{3,6},{2,7},{9,8},{8,9},{13,10... | collective-permute-start | bytes 393224 | tf_op jit(solution)/shard_map/ppermute | solution.py:854
  203.1 20.3 %attn_fwd.2 = (bf16[512,128]{1,0:T(8,128)(2,1)}, bf16[512,128]{1,0:T(8,128)(2,1)}, bf16[512,128]{1,0:T(8,128)(2,1)}, bf16[512,128]{1,0:T(8,128)(2,1)}, bf16[2,20...) custom-call(s32[4]{0:T(128)} %pad_add_fusion.1.s_ref, bf16[2048,256]{1,0:T(8,128)(2,1)} %get-tuple-element.68.refs_0_, ...), custom_call_target="tpu_custom_call" | custom-call | flops 8589934592 | bytes 4194304 | tf_op jit(solution)/shard_map/attn_fwd/pallas_call | solution.py:233
  225.4 4.4 collective-permute-start.3
  237.2 3.3 collective-permute-done.5.refs_4_
  241.2 6.5 %middle.1 = (f32[512,1024]{1,0:T(8,128)}, bf16[512,1024]{1,0:T(8,128)(2,1)}, f32[8,1024]{1,0:T(8,128)}) custom-call(s32[4]{0:T(128)} %pad_add_fusion.1.s_ref, bf16[512,128]{1,0:T(8,128)(2,1)} %copy-done.22, bf16[512,128]{1,0:T(8,128)(2,1)} %copy-done.18, bf16[512,128]{1,0:T(8,128)(2,1)} %copy-done.23, bf16[512,128]{1,0:T(8,128)(2,1)} %copy-done.19, ...), custom_call_target="tpu_custom_call" | custom-call | flops 1073741824 | bytes 8388608 | tf_op jit(solution)/shard_map/middle/pallas_call | solution.py:381
  247.7 36.4 %ffn.1 = (f32[512,1024]{1,0:T(8,128)}, f32[512,1024]{1,0:T(8,128)}, bf16[4,4,1968,128]{3,2,1,0:T(8,128)(2,1)}, bf16[4,4,1968,128]{3,2,1,0:T(8,128)(2,1)}) custom-call(s32[4]{0:T(128)} %pad_add_fusion.1.s_ref, bf16[512,1024]{1,0:T(8,128)(2,1)} %get-tuple-element.81.x_ref, bf16[512,1024]{1,0:T(8,128)(2,1)} %grad_ref.1, ...), custom_call_target="tpu_custom_call" | custom-call | flops 24763170816 | bytes 41943040 | tf_op jit(solution)/shard_map/ffn/pallas_call | solution.py:534
  284.9 9.1 %middle_back.1 = (bf16[512,1024]{1,0:T(8,128)(2,1)}, f32[512,1024]{1,0:T(8,128)}, bf16[512,1024]{1,0:T(8,128)(2,1)}, f32[8,1024]{1,0:T(8,128)}, bf16[512,128]{1,...) custom-call(s32[4]{0:T(128)} %pad_add_fusion.1.s_ref, ...), custom_call_target="tpu_custom_call" | custom-call | flops 1073741824 | bytes 12582912 | tf_op jit(solution)/shard_map/middle_back/pallas_call | solution.py:432
  300.7 3.5 fusion.60
  304.2 5.0 attn_grad.1
  330.1 6.3 %collective-permute-done.39 = bf16[2,2,256,128]{2,3,1,0:T(8,128)(2,1)S(1)} collective-permute-done((bf16[2,2,256,128]{2,3,1,0:T(8,128)(2,1)S(1)}, bf16[2,2,256,128]{2,3,1,0:T(8,128)(2,1)S(1)}, u32[]{:S(2)}, u32[]{:S(2)}) %collective-permute-start.39) | collective-permute-done | bytes 262176 | tf_op jit(solution)/shard_map/ppermute | solution.py:843
  338.1 3.5 collective-permute-start.12
  343.0 3.7 collective-permute-done.38
  346.7 3.5 collective-permute-start.13
  351.0 3.8 fusion.61
  364.7 30.9 %attn_bwd.2 = (bf16[512,384]{1,0:T(8,128)(2,1)}, bf16[512,384]{1,0:T(8,128)(2,1)}, bf16[512,384]{1,0:T(8,128)(2,1)}, bf16[512,384]{1,0:T(8,128)(2,1)}) custom-call(s32[4]{0:T(128)} %pad_add_fusion.1.s_ref, bf16[2,2048,128]{2,1,0:T(8,128)(2,1)} %get-tuple-element.86.refs_0_, bf16[2,2048,128]{2,1,0:T(8,128)(2,1)} %get-tuple-element.87.refs_1_, ...), custom_call_target="tpu_custom_call" | custom-call | flops 15032385536 | bytes 8388608 | tf_op jit(solution)/shard_map/attn_bwd/pallas_call | solution.py:335
  395.5 6.3 %qkv_grad.2 = (bf16[4,384,128]{2,1,0:T(8,128)(2,1)}, bf16[4,384,128]{2,1,0:T(8,128)(2,1)}) custom-call(s32[4]{0:T(128)} %pad_add_fusion.1.s_ref, bf16[512,384]{1,0:T(8,128)(2,1)} %get-tuple-element.95.refs_0_, bf16[512,384]{1,0:T(8,128)(2,1)} %get-tuple-element.107.refs_1_, bf16[512,384]{1,0:T(8,128)(2,1)} %get-tuple-element.109.refs_2_, ...), custom_call_target="tpu_custom_call" | custom-call | flops 1610612736 | bytes 7340032 | tf_op jit(solution)/shard_map/qkv_grad/pallas_call | solution.py:573
  409.5 7.2 %collective-permute-done.29 = bf16[4,384,128]{2,1,0:T(8,128)(2,1)S(1)} collective-permute-done((bf16[4,384,128]{2,1,0:T(8,128)(2,1)}, bf16[4,384,128]{2,1,0:T(8,128)(2,1)S(1)}, u32[]{:S(2)}, u32[]{:S(2)}) %collective-permute-start.29) | collective-permute-done | bytes 393248 | tf_op jit(solution)/shard_map/ppermute | solution.py:843
  416.7 3.3 collective-permute-start.20
  433.2 31.0 %attn_bwd.3 = (bf16[512,384]{1,0:T(8,128)(2,1)}, bf16[512,384]{1,0:T(8,128)(2,1)}, bf16[512,384]{1,0:T(8,128)(2,1)}, bf16[512,384]{1,0:T(8,128)(2,1)}) custom-call(s32[4]{0:T(128)} %pad_add_fusion.1.s_ref, bf16[2,2048,128]{2,1,0:T(8,128)(2,1)} %get-tuple-element.96.refs_0_, bf16[2,2048,128]{2,1,0:T(8,128)(2,1)} %get-tuple-element.97.refs_1_, ...), custom_call_target="tpu_custom_call" | custom-call | flops 15032385536 | bytes 8388608 | tf_op jit(solution)/shard_map/attn_bwd/pallas_call | solution.py:335
  466.2 3.5 collective-permute-start.24
  472.0 6.3 %qkv_grad.3 = (bf16[4,384,128]{2,1,0:T(8,128)(2,1)}, bf16[4,384,128]{2,1,0:T(8,128)(2,1)}) custom-call(s32[4]{0:T(128)} %pad_add_fusion.1.s_ref, bf16[512,384]{1,0:T(8,128)(2,1)} %get-tuple-element.106.refs_0_, bf16[512,384]{1,0:T(8,128)(2,1)} %get-tuple-element.108.refs_1_, bf16[512,384]{1,0:T(8,128)(2,1)} %get-tuple-element.110.refs_2_, ...), custom_call_target="tpu_custom_call" | custom-call | flops 1610612736 | bytes 7340032 | tf_op jit(solution)/shard_map/qkv_grad/pallas_call | solution.py:573
  480.2 8.2 %collective-permute-done.22.refs_1_ = bf16[512,384]{1,0:T(8,128)(2,1)S(1)} collective-permute-done((bf16[512,384]{1,0:T(8,128)(2,1)}, bf16[512,384]{1,0:T(8,128)(2,1)S(1)}, u32[]{:S(2)}, u32[]{:S(2)}) %collective-permute-start.22) | collective-permute-done | bytes 393248 | tf_op jit(solution)/shard_map/ppermute | solution.py:854
  490.3 10.4 %collective-permute-done.26.refs_5_ = bf16[512,384]{1,0:T(8,128)(2,1)S(1)} collective-permute-done((bf16[512,384]{1,0:T(8,128)(2,1)}, bf16[512,384]{1,0:T(8,128)(2,1)S(1)}, u32[]{:S(2)}, u32[]{:S(2)}) %collective-permute-start.26) | collective-permute-done | bytes 393248 | tf_op jit(solution)/shard_map/ppermute | solution.py:854
  502.1 12.1 %input_grad.1 = (f32[512,1024]{1,0:T(8,128)}, f32[1,1024]{1,0:T(1,128)}) custom-call(s32[4]{0:T(128)} %pad_add_fusion.1.s_ref, bf16[512,384]{1,0:T(8,128)(2,1)} %copy-done.5, bf16[512,384]{1,0:T(8,128)(2,1)} %copy-done.9, bf16[512,384]{1,0:T(8,128)(2,1)} %copy-done.6, bf16[512,384]{1,0:T(8,128)(2,1)} %copy-done.10, bf16[512,384]{1,0:T(8,128)(2,1)} %copy-done.7, ...), custom_call_target="tpu_custom_call" | custom-call | flops 3221225472 | bytes 14680064 | tf_op jit(solution)/shard_map/input_grad/pallas_call | solution.py:603
  524.7 7.6 %collective-permute-start.58 = (f32[1,1024]{1,0:T(1,128)S(1)}, f32[1,1024]{1,0:T(1,128)S(1)}, u32[]{:S(2)}, u32[]{:S(2)}) collective-permute-start(f32[1,1024]{1,0:T(1,128)S(1)} %add_add_fusion.3), channel_id=1, source_target_pairs={{0,3},{1,0},{2,1},{3,2},{4,7},{5,4},{6,5},{7,6},{8,11},{9,8},{10,9... | collective-permute-start | bytes 12296 | tf_op jit(solution)/shard_map/ppermute | solution.py:908
  541.1 4.9 collective-permute-done.45
  552.3 7.3 %collective-permute-start.47 = (bf16[1968,128]{1,0:T(8,128)(2,1)S(1)}, bf16[1968,128]{1,0:T(8,128)(2,1)}, u32[]{:S(2)}, u32[]{:S(2)}) collective-permute-start(bf16[1968,128]{1,0:T(8,128)(2,1)S(1)} %get-tuple-element.157), channel_id=1, source_target_pairs={{0,2},{1,3},{2,0},{3,1},{4,6},{5,7},{6,4},{7,5},{8,10},{9,11},{10,... | collective-permute-start | bytes 1511432 | tf_op jit(solution)/shard_map/ppermute | solution.py:892
  566.3 37.5 %collective-permute-done.47 = bf16[1968,128]{1,0:T(8,128)(2,1)} collective-permute-done((bf16[1968,128]{1,0:T(8,128)(2,1)S(1)}, bf16[1968,128]{1,0:T(8,128)(2,1)}, u32[]{:S(2)}, u32[]{:S(2)}) %collective-permute-start.47) | collective-permute-done | bytes 503840 | tf_op jit(solution)/shard_map/ppermute | solution.py:892
  (296 shorter events, 130.7 us)
Async XLA Ops:
  0.7 150.9 %collective-permute-start = (s32[2048]{0:T(1024)}, s32[2048]{0:T(1024)S(1)}, u32[]{:S(2)}, u32[]{:S(2)}) collective-permute-start(s32[2048]{0:T(1024)} %bitcast.206), channel_id=1, source_target_pairs={{0,4},{4,0},{8,12},{12,8},{16,20},{20,16},{24,28},{28,24},{1,5},{5... | collective-permute-start | bytes 24584 | tf_op jit(solution)/shard_map/ppermute | solution.py:843
  191.5 33.9 %collective-permute-start.2 = (bf16[512,128]{1,0:T(8,128)(2,1)}, bf16[512,128]{1,0:T(8,128)(2,1)S(1)}, u32[]{:S(2)}, u32[]{:S(2)}) collective-permute-start(bf16[512,128]{1,0:T(8,128)(2,1)} %get-tuple-element.72.refs_7_), channel_id=1, source_target_pairs={{0,0},{1,1},{4,2},{5,3},{6,4},{7,5},{2,6},{3,7},{8,8},{9,9},{12,10... | collective-permute-start | bytes 393224 | tf_op jit(solution)/shard_map/ppermute | solution.py:854
  193.8 36.0 %collective-permute-start.4 = (bf16[512,128]{1,0:T(8,128)(2,1)}, bf16[512,128]{1,0:T(8,128)(2,1)S(1)}, u32[]{:S(2)}, u32[]{:S(2)}) collective-permute-start(bf16[512,128]{1,0:T(8,128)(2,1)} %get-tuple-element.74.refs_8_), channel_id=1, source_target_pairs={{1,0},{0,1},{5,2},{4,3},{7,4},{6,5},{3,6},{2,7},{9,8},{8,9},{13,10... | collective-permute-start | bytes 393224 | tf_op jit(solution)/shard_map/ppermute | solution.py:854
  201.0 30.7 %collective-permute-start.6 = (bf16[512,128]{1,0:T(8,128)(2,1)}, bf16[512,128]{1,0:T(8,128)(2,1)S(1)}, u32[]{:S(2)}, u32[]{:S(2)}) collective-permute-start(bf16[512,128]{1,0:T(8,128)(2,1)} %get-tuple-element.76.refs_9_), channel_id=1, source_target_pairs={{4,0},{5,1},{0,2},{1,3},{2,4},{3,5},{6,6},{7,7},{12,8},{13,9},{8,1... | collective-permute-start | bytes 393224 | tf_op jit(solution)/shard_map/ppermute | solution.py:854
  284.1 66.8 %collective-permute-start.10 = (bf16[4,4,1968,128]{3,2,1,0:T(8,128)(2,1)}, bf16[4,4,1968,128]{3,2,1,0:T(8,128)(2,1)}, u32[]{:S(2)}, u32[]{:S(2)}) collective-permute-start(bf16[4,4,1968,128]{3,2,1,0:T(8,128)(2,1)} %get-tuple-element.90), channel_id=1, source_target_pairs={{0,4},{4,0},{8,12},{12,8},{16,20},{20,16},{24,28},{28,24},{1,5},{5... | collective-permute-start | bytes 24182792 | tf_op jit(solution)/shard_map/ppermute | solution.py:843
  322.8 37.5 %collective-permute-start.9 = (bf16[512,128]{1,0:T(8,128)(2,1)}, bf16[512,128]{1,0:T(8,128)(2,1)}, u32[]{:S(2)}, u32[]{:S(2)}) collective-permute-start(bf16[512,128]{1,0:T(8,128)(2,1)} %get-tuple-element.88), channel_id=1, source_target_pairs={{0,0},{1,1},{2,4},{3,5},{4,6},{5,7},{6,2},{7,3},{8,8},{9,9},{10,12... | collective-permute-start | bytes 393224 | tf_op jit(solution)/shard_map/ppermute | solution.py:854
  324.7 36.0 %collective-permute-start.11 = (bf16[512,128]{1,0:T(8,128)(2,1)}, bf16[512,128]{1,0:T(8,128)(2,1)}, u32[]{:S(2)}, u32[]{:S(2)}) collective-permute-start(bf16[512,128]{1,0:T(8,128)(2,1)} %get-tuple-element.92), channel_id=1, source_target_pairs={{0,1},{1,0},{2,5},{3,4},{4,7},{5,6},{6,3},{7,2},{8,9},{9,8},{10,13... | collective-permute-start | bytes 393224 | tf_op jit(solution)/shard_map/ppermute | solution.py:854
  338.1 24.7 %collective-permute-start.12 = (bf16[512,128]{1,0:T(8,128)(2,1)}, bf16[512,128]{1,0:T(8,128)(2,1)}, u32[]{:S(2)}, u32[]{:S(2)}) collective-permute-start(bf16[512,128]{1,0:T(8,128)(2,1)} %get-tuple-element.93), channel_id=1, source_target_pairs={{0,4},{1,5},{2,0},{3,1},{4,2},{5,3},{6,6},{7,7},{8,12},{9,13},{10,... | collective-permute-start | bytes 393224 | tf_op jit(solution)/shard_map/ppermute | solution.py:854
  350.9 50.9 %collective-permute-start.41 = (bf16[256,128]{0,1:T(8,128)(2,1)}, bf16[256,128]{0,1:T(8,128)(2,1)}, u32[]{:S(2)}, u32[]{:S(2)}) collective-permute-start(bf16[256,128]{0,1:T(8,128)(2,1)} %get-tuple-element.173), channel_id=1, source_target_pairs={{0,1},{1,2},{2,3},{3,0},{4,5},{5,6},{6,7},{7,4},{8,9},{9,10},{10,1... | collective-permute-start | bytes 196616 | tf_op jit(solution)/shard_map/ppermute | solution.py:892
  360.3 43.4 %collective-permute-start.42 = (bf16[256,128]{0,1:T(8,128)(2,1)}, bf16[256,128]{0,1:T(8,128)(2,1)}, u32[]{:S(2)}, u32[]{:S(2)}) collective-permute-start(bf16[256,128]{0,1:T(8,128)(2,1)} %get-tuple-element.174), channel_id=1, source_target_pairs={{0,2},{1,3},{2,0},{3,1},{4,6},{5,7},{6,4},{7,5},{8,10},{9,11},{10,... | collective-permute-start | bytes 196616 | tf_op jit(solution)/shard_map/ppermute | solution.py:892
  360.7 44.9 %collective-permute-start.43 = (bf16[256,128]{0,1:T(8,128)(2,1)}, bf16[256,128]{0,1:T(8,128)(2,1)}, u32[]{:S(2)}, u32[]{:S(2)}) collective-permute-start(bf16[256,128]{0,1:T(8,128)(2,1)} %get-tuple-element.175), channel_id=1, source_target_pairs={{0,3},{1,0},{2,1},{3,2},{4,7},{5,4},{6,5},{7,6},{8,11},{9,8},{10,9... | collective-permute-start | bytes 196616 | tf_op jit(solution)/shard_map/ppermute | solution.py:892
  362.8 57.3 %collective-permute-start.16 = (bf16[2,2,1968,128]{3,2,1,0:T(8,128)(2,1)}, bf16[2,2,1968,128]{3,2,1,0:T(8,128)(2,1)}, u32[]{:S(2)}, u32[]{:S(2)}) collective-permute-start(bf16[2,2,1968,128]{3,2,1,0:T(8,128)(2,1)} %fusion.1), channel_id=1, source_target_pairs={{0,8},{4,12},{8,0},{12,4},{16,24},{20,28},{24,16},{28,20},{1,9},{5... | collective-permute-start | bytes 6045704 | tf_op jit(solution)/shard_map/ppermute | solution.py:843
  363.3 59.4 %collective-permute-start.17 = (bf16[2,2,1968,128]{3,2,1,0:T(8,128)(2,1)}, bf16[2,2,1968,128]{3,2,1,0:T(8,128)(2,1)}, u32[]{:S(2)}, u32[]{:S(2)}) collective-permute-start(bf16[2,2,1968,128]{3,2,1,0:T(8,128)(2,1)} %get-tuple-element.151), channel_id=1, source_target_pairs={{0,16},{4,20},{8,24},{12,28},{16,0},{20,4},{24,8},{28,12},{1,17},{... | collective-permute-start | bytes 6045704 | tf_op jit(solution)/shard_map/ppermute | solution.py:843
  401.8 24.4 %collective-permute-start.15 = (bf16[512,128]{1,0:T(8,128)(2,1)}, bf16[512,128]{1,0:T(8,128)(2,1)S(1)}, u32[]{:S(2)}, u32[]{:S(2)}) collective-permute-start(bf16[512,128]{1,0:T(8,128)(2,1)} %get-tuple-element.98), channel_id=1, source_target_pairs={{0,0},{1,1},{2,4},{3,5},{4,6},{5,7},{6,2},{7,3},{8,8},{9,9},{10,12... | collective-permute-start | bytes 393224 | tf_op jit(solution)/shard_map/ppermute | solution.py:854
  403.7 25.4 %collective-permute-start.19 = (bf16[512,128]{1,0:T(8,128)(2,1)}, bf16[512,128]{1,0:T(8,128)(2,1)S(1)}, u32[]{:S(2)}, u32[]{:S(2)}) collective-permute-start(bf16[512,128]{1,0:T(8,128)(2,1)} %get-tuple-element.103), channel_id=1, source_target_pairs={{0,1},{1,0},{2,5},{3,4},{4,7},{5,6},{6,3},{7,2},{8,9},{9,8},{10,13... | collective-permute-start | bytes 393224 | tf_op jit(solution)/shard_map/ppermute | solution.py:854
  422.7 41.6 %collective-permute-start.14 = (bf16[512,384]{1,0:T(8,128)(2,1)S(1)}, bf16[512,384]{1,0:T(8,128)(2,1)S(1)}, u32[]{:S(2)}, u32[]{:S(2)}) collective-permute-start(bf16[512,384]{1,0:T(8,128)(2,1)S(1)} %copy-done.30), channel_id=1, source_target_pairs={{0,0},{1,1},{4,2},{5,3},{6,4},{7,5},{2,6},{3,7},{8,8},{9,9},{12,10... | collective-permute-start | bytes 1179656 | tf_op jit(solution)/shard_map/ppermute | solution.py:854
  426.3 39.9 %collective-permute-start.23 = (bf16[512,384]{1,0:T(8,128)(2,1)S(1)}, bf16[512,384]{1,0:T(8,128)(2,1)S(1)}, u32[]{:S(2)}, u32[]{:S(2)}) collective-permute-start(bf16[512,384]{1,0:T(8,128)(2,1)S(1)} %copy-done.29), channel_id=1, source_target_pairs={{1,0},{0,1},{5,2},{4,3},{7,4},{6,5},{3,6},{2,7},{9,8},{8,9},{13,10... | collective-permute-start | bytes 1179656 | tf_op jit(solution)/shard_map/ppermute | solution.py:854
  429.2 40.5 %collective-permute-start.25 = (bf16[512,384]{1,0:T(8,128)(2,1)S(1)}, bf16[512,384]{1,0:T(8,128)(2,1)S(1)}, u32[]{:S(2)}, u32[]{:S(2)}) collective-permute-start(bf16[512,384]{1,0:T(8,128)(2,1)S(1)} %copy-done.28), channel_id=1, source_target_pairs={{4,0},{5,1},{0,2},{1,3},{2,4},{3,5},{6,6},{7,7},{12,8},{13,9},{8,1... | collective-permute-start | bytes 1179656 | tf_op jit(solution)/shard_map/ppermute | solution.py:854
  431.1 47.2 %collective-permute-start.27 = (bf16[512,384]{1,0:T(8,128)(2,1)}, bf16[512,384]{1,0:T(8,128)(2,1)S(1)}, u32[]{:S(2)}, u32[]{:S(2)}) collective-permute-start(bf16[512,384]{1,0:T(8,128)(2,1)} %get-tuple-element.111.refs_3_), channel_id=1, source_target_pairs={{5,0},{4,1},{1,2},{0,3},{3,4},{2,5},{7,6},{6,7},{13,8},{12,9},{9,1... | collective-permute-start | bytes 1179656 | tf_op jit(solution)/shard_map/ppermute | solution.py:854
  432.1 39.6 %collective-permute-start.30 = (bf16[2,384,128]{2,1,0:T(8,128)(2,1)S(1)}, bf16[2,384,128]{2,1,0:T(8,128)(2,1)S(1)}, u32[]{:S(2)}, u32[]{:S(2)}) collective-permute-start(bf16[2,384,128]{2,1,0:T(8,128)(2,1)S(1)} %fusion.34), channel_id=1, source_target_pairs={{0,16},{4,20},{8,24},{12,28},{16,0},{20,4},{24,8},{28,12},{1,17},{... | collective-permute-start | bytes 589832 | tf_op jit(solution)/shard_map/ppermute | solution.py:843
  464.3 24.1 %collective-permute-start.22 = (bf16[512,384]{1,0:T(8,128)(2,1)}, bf16[512,384]{1,0:T(8,128)(2,1)S(1)}, u32[]{:S(2)}, u32[]{:S(2)}) collective-permute-start(bf16[512,384]{1,0:T(8,128)(2,1)} %get-tuple-element.106.refs_0_), channel_id=1, source_target_pairs={{0,0},{1,1},{4,2},{5,3},{6,4},{7,5},{2,6},{3,7},{8,8},{9,9},{12,10... | collective-permute-start | bytes 1179656 | tf_op jit(solution)/shard_map/ppermute | solution.py:854
  469.7 31.0 %collective-permute-start.26 = (bf16[512,384]{1,0:T(8,128)(2,1)}, bf16[512,384]{1,0:T(8,128)(2,1)S(1)}, u32[]{:S(2)}, u32[]{:S(2)}) collective-permute-start(bf16[512,384]{1,0:T(8,128)(2,1)} %get-tuple-element.110.refs_2_), channel_id=1, source_target_pairs={{4,0},{5,1},{0,2},{1,3},{2,4},{3,5},{6,6},{7,7},{12,8},{13,9},{8,1... | collective-permute-start | bytes 1179656 | tf_op jit(solution)/shard_map/ppermute | solution.py:854
  471.6 30.4 %collective-permute-start.28 = (bf16[512,384]{1,0:T(8,128)(2,1)}, bf16[512,384]{1,0:T(8,128)(2,1)}, u32[]{:S(2)}, u32[]{:S(2)}) collective-permute-start(bf16[512,384]{1,0:T(8,128)(2,1)} %get-tuple-element.112.refs_3_), channel_id=1, source_target_pairs={{5,0},{4,1},{1,2},{0,3},{3,4},{2,5},{7,6},{6,7},{13,8},{12,9},{9,1... | collective-permute-start | bytes 1179656 | tf_op jit(solution)/shard_map/ppermute | solution.py:854
  478.3 35.9 %collective-permute-start.31 = (bf16[384,128]{1,0:T(8,128)(2,1)S(1)}, bf16[384,128]{1,0:T(8,128)(2,1)S(1)}, u32[]{:S(2)}, u32[]{:S(2)}) collective-permute-start(bf16[384,128]{1,0:T(8,128)(2,1)S(1)} %get-tuple-element.176), channel_id=1, source_target_pairs={{0,0},{1,1},{2,6},{3,7},{4,2},{5,3},{6,4},{7,5},{8,8},{9,9},{10,14... | collective-permute-start | bytes 294920 | tf_op jit(solution)/shard_map/ppermute | solution.py:1035
  488.4 27.1 %collective-permute-start.32 = (bf16[384,128]{1,0:T(8,128)(2,1)S(1)}, bf16[384,128]{1,0:T(8,128)(2,1)S(1)}, u32[]{:S(2)}, u32[]{:S(2)}) collective-permute-start(bf16[384,128]{1,0:T(8,128)(2,1)S(1)} %get-tuple-element.177), channel_id=1, source_target_pairs={{0,4},{1,5},{2,2},{3,3},{4,6},{5,7},{6,0},{7,1},{8,12},{9,13},{10,... | collective-permute-start | bytes 294920 | tf_op jit(solution)/shard_map/ppermute | solution.py:1035
  489.1 48.2 %collective-permute-start.44 = (bf16[2,1968,128]{2,1,0:T(8,128)(2,1)S(1)}, bf16[2,1968,128]{2,1,0:T(8,128)(2,1)S(1)}, u32[]{:S(2)}, u32[]{:S(2)}) collective-permute-start(bf16[2,1968,128]{2,1,0:T(8,128)(2,1)S(1)} %fusion.9), channel_id=1, source_target_pairs={{0,16},{4,20},{8,24},{12,28},{16,0},{20,4},{24,8},{28,12},{1,17},{... | collective-permute-start | bytes 3022856 | tf_op jit(solution)/shard_map/ppermute | solution.py:843
  520.9 25.1 %collective-permute-start.45 = (bf16[2,1968,128]{2,1,0:T(8,128)(2,1)S(1)}, bf16[2,1968,128]{2,1,0:T(8,128)(2,1)S(1)}, u32[]{:S(2)}, u32[]{:S(2)}) collective-permute-start(bf16[2,1968,128]{2,1,0:T(8,128)(2,1)S(1)} %fusion.10), channel_id=1, source_target_pairs={{0,8},{4,12},{8,0},{12,4},{16,24},{20,28},{24,16},{28,20},{1,9},{5... | collective-permute-start | bytes 3022856 | tf_op jit(solution)/shard_map/ppermute | solution.py:843
  524.7 24.9 %collective-permute-start.58 = (f32[1,1024]{1,0:T(1,128)S(1)}, f32[1,1024]{1,0:T(1,128)S(1)}, u32[]{:S(2)}, u32[]{:S(2)}) collective-permute-start(f32[1,1024]{1,0:T(1,128)S(1)} %add_add_fusion.3), channel_id=1, source_target_pairs={{0,3},{1,0},{2,1},{3,2},{4,7},{5,4},{6,5},{7,6},{8,11},{9,8},{10,9... | collective-permute-start | bytes 12296 | tf_op jit(solution)/shard_map/ppermute | solution.py:908
  533.4 26.1 %collective-permute-start.56 = (f32[1,1024]{1,0:T(1,128)S(1)}, f32[1,1024]{1,0:T(1,128)S(1)}, u32[]{:S(2)}, u32[]{:S(2)}) collective-permute-start(f32[1,1024]{1,0:T(1,128)S(1)} %add_add_fusion.3), channel_id=1, source_target_pairs={{0,1},{1,2},{2,3},{3,0},{4,5},{5,6},{6,7},{7,4},{8,9},{9,10},{10,1... | collective-permute-start | bytes 12296 | tf_op jit(solution)/shard_map/ppermute | solution.py:908
  537.3 24.8 %collective-permute-start.35 = (bf16[384,128]{1,0:T(8,128)(2,1)S(1)}, bf16[384,128]{1,0:T(8,128)(2,1)S(1)}, u32[]{:S(2)}, u32[]{:S(2)}) collective-permute-start(bf16[384,128]{1,0:T(8,128)(2,1)S(1)} %get-tuple-element.178), channel_id=1, source_target_pairs={{0,0},{1,1},{2,6},{3,7},{4,2},{5,3},{6,4},{7,5},{8,8},{9,9},{10,14... | collective-permute-start | bytes 294920 | tf_op jit(solution)/shard_map/ppermute | solution.py:1035
  552.3 51.6 %collective-permute-start.47 = (bf16[1968,128]{1,0:T(8,128)(2,1)S(1)}, bf16[1968,128]{1,0:T(8,128)(2,1)}, u32[]{:S(2)}, u32[]{:S(2)}) collective-permute-start(bf16[1968,128]{1,0:T(8,128)(2,1)S(1)} %get-tuple-element.157), channel_id=1, source_target_pairs={{0,2},{1,3},{2,0},{3,1},{4,6},{5,7},{6,4},{7,5},{8,10},{9,11},{10,... | collective-permute-start | bytes 1511432 | tf_op jit(solution)/shard_map/ppermute | solution.py:892
  559.5 44.3 %collective-permute-start.48 = (bf16[1968,128]{1,0:T(8,128)(2,1)S(1)}, bf16[1968,128]{1,0:T(8,128)(2,1)}, u32[]{:S(2)}, u32[]{:S(2)}) collective-permute-start(bf16[1968,128]{1,0:T(8,128)(2,1)S(1)} %get-tuple-element.158), channel_id=1, source_target_pairs={{0,3},{1,0},{2,1},{3,2},{4,7},{5,4},{6,5},{7,6},{8,11},{9,8},{10,9... | collective-permute-start | bytes 1511432 | tf_op jit(solution)/shard_map/ppermute | solution.py:892
  (77 other events, 956.7 us)
